TPU v7x, 16 devices: a whole 2x2x2 slice. The times are simulated.
16 devices in a mesh: data: 16 (over z, y, x, core).
Axes of the slice: x: 2, y: 2, z: 2, core: 2. Of those that a mesh axis runs over, the one named last changes fastest.
Arguments:
- act_in: bfloat16 [65536, 896], P('data')
- grad_out: bfloat16 [65536, 896], P('data')
- w_up: bfloat16 [2, 896, 4864], replicated
- w_down: bfloat16 [2, 4864, 896], replicated
- master_up: float32 [2, 896, 4864], P(None, 'data')
- master_down: float32 [2, 4864, 896], P(None, 'data')
- exp_avg_up: float32 [2, 896, 4864], P(None, 'data')
- exp_avg_down: float32 [2, 4864, 896], P(None, 'data')
- exp_sq_up: float32 [2, 896, 4864], P(None, 'data')
- exp_sq_down: float32 [2, 4864, 896], P(None, 'data')
- learn_rate: float32 [], replicated
- clip_norm: float32 [], replicated
Outputs:
- output 1: bfloat16 [2, 896, 4864], replicated
- output 2: bfloat16 [2, 4864, 896], replicated
- output 3: float32 [2, 896, 4864], P(None, 'data')
- output 4: float32 [2, 4864, 896], P(None, 'data')
- output 5: float32 [2, 896, 4864], P(None, 'data')
- output 6: float32 [2, 4864, 896], P(None, 'data')
- output 7: float32 [2, 896, 4864], P(None, 'data')
- output 8: float32 [2, 4864, 896], P(None, 'data')
- output 9: float32 [], replicated
All inputs are finite; a program needn't handle non-finite values.
Results may differ from a plain program's by a relative error of at most 0.00407.
Values are sent between devices in bfloat16 or wider.
A program may use at most 1 GiB of HBM per device.

v0:
```python
import jax
import jax.numpy as jnp
from jax import lax
from jax.sharding import PartitionSpec as P

STEP = 10
BETA_ONE = 0.9
BETA_TWO = 0.95
ADAM_EPS = 1e-8
NORM_EPS = 1e-6
INV_SQRT_TWO = 0.7071067811865476
INV_SQRT_TWO_PI = 0.3989422804014327


def gelu_parts(pre_act):
    normal_cdf = 0.5 * (1.0 + lax.erf(pre_act * INV_SQRT_TWO))
    normal_pdf = jnp.exp(-0.5 * pre_act * pre_act) * INV_SQRT_TWO_PI
    return pre_act * normal_cdf, normal_cdf + pre_act * normal_pdf


def local_grads(act_in, grad_out, w_up, w_down):
    z_one = jnp.einsum("td,df->tf", act_in, w_up[0], preferred_element_type=jnp.float32)
    gelu_one, slope_one = gelu_parts(z_one)
    act_one = gelu_one.astype(jnp.bfloat16)
    hidden = jnp.einsum("tf,fd->td", act_one, w_down[0], preferred_element_type=jnp.float32).astype(jnp.bfloat16)
    z_three = jnp.einsum("td,df->tf", hidden, w_up[1], preferred_element_type=jnp.float32)
    gelu_three, slope_three = gelu_parts(z_three)
    act_three = gelu_three.astype(jnp.bfloat16)
    g_four = jnp.einsum("tf,td->fd", act_three, grad_out, preferred_element_type=jnp.float32)
    dz_three = (jnp.einsum("td,fd->tf", grad_out, w_down[1], preferred_element_type=jnp.float32) * slope_three).astype(jnp.bfloat16)
    g_three = jnp.einsum("td,tf->df", hidden, dz_three, preferred_element_type=jnp.float32)
    d_hidden = jnp.einsum("tf,df->td", dz_three, w_up[1], preferred_element_type=jnp.float32).astype(jnp.bfloat16)
    g_two = jnp.einsum("tf,td->fd", act_one, d_hidden, preferred_element_type=jnp.float32)
    dz_one = (jnp.einsum("td,fd->tf", d_hidden, w_down[0], preferred_element_type=jnp.float32) * slope_one).astype(jnp.bfloat16)
    g_one = jnp.einsum("td,tf->df", act_in, dz_one, preferred_element_type=jnp.float32)
    return g_one, g_two, g_three, g_four


def adam_direction(exp_avg, exp_sq, grad, clip_scale):
    bias_one = 1.0 - BETA_ONE ** STEP
    bias_two = 1.0 - BETA_TWO ** STEP
    avg_new = BETA_ONE * exp_avg + (1.0 - BETA_ONE) * clip_scale * grad
    sq_new = BETA_TWO * exp_sq + (1.0 - BETA_TWO) * (clip_scale * clip_scale) * (grad * grad)
    direction = (avg_new / bias_one) / (jnp.sqrt(sq_new / bias_two) + ADAM_EPS)
    return avg_new, sq_new, direction


def sum_squares(stacked):
    return jnp.sum(stacked * stacked, axis=(1, 2))


def solution(mesh):
    group_size = mesh.shape["data"]
    batch_rows = P("data", None)
    state_rows = P(None, "data", None)
    replicated = P()

    def reduce_rows(grad):
        return lax.psum_scatter(grad, "data", scatter_dimension=0, tiled=True) / group_size

    def device_step(act_in, grad_out, w_up, w_down, master_up, master_down, exp_avg_up, exp_avg_down, exp_sq_up, exp_sq_down, learn_rate, clip_norm):
        g_one, g_two, g_three, g_four = local_grads(act_in, grad_out, w_up, w_down)
        shard_four = reduce_rows(g_four)
        shard_three = reduce_rows(g_three)
        shard_two = reduce_rows(g_two)
        shard_one = reduce_rows(g_one)
        grad_up = jnp.stack([shard_one, shard_three])
        grad_down = jnp.stack([shard_two, shard_four])
        local_sq = jnp.sum(grad_up * grad_up) + jnp.sum(grad_down * grad_down)
        grad_norm = jnp.sqrt(lax.psum(local_sq, "data"))
        clip_scale = jnp.minimum(1.0, clip_norm / (grad_norm + NORM_EPS))
        avg_up, sq_up, dir_up = adam_direction(exp_avg_up, exp_sq_up, grad_up, clip_scale)
        avg_down, sq_down, dir_down = adam_direction(exp_avg_down, exp_sq_down, grad_down, clip_scale)
        local_stats = jnp.concatenate([sum_squares(master_up), sum_squares(master_down), sum_squares(dir_up), sum_squares(dir_down)])
        norm_stats = lax.psum(local_stats, "data")
        trust_ratio = jnp.sqrt(norm_stats[0:4]) / jnp.sqrt(norm_stats[4:8])
        master_up_out = master_up - learn_rate * trust_ratio[0:2, None, None] * dir_up
        master_down_out = master_down - learn_rate * trust_ratio[2:4, None, None] * dir_down
        new_w_up = lax.all_gather(master_up_out.astype(jnp.bfloat16), "data", axis=1, tiled=True)
        new_w_down = lax.all_gather(master_down_out.astype(jnp.bfloat16), "data", axis=1, tiled=True)
        return (new_w_up, new_w_down, master_up_out, master_down_out, avg_up, avg_down, sq_up, sq_down, grad_norm)

    return jax.shard_map(device_step, mesh=mesh, in_specs=(batch_rows, batch_rows, replicated, replicated, state_rows, state_rows, state_rows, state_rows, state_rows, state_rows, replicated, replicated), out_specs=(replicated, replicated, state_rows, state_rows, state_rows, state_rows, state_rows, state_rows, replicated), check_vma=False)
```

profile of v0, /device:TPU:0, one launch (start us, length us, event | category | flops | bytes accessed | tf_op | source)
XLA Modules:
  0.0 1305.8 jit_solution(12183412199681952263)
XLA Ops:
  7.2 0.0 reduce-scatter.15.cloned.1.call-start
  7.2 59.4 %multiply_convert_fusion.1 = (bf16[4096,4864]{1,0:T(8,128)(2,1)}, f32[4096,4864]{1,0:T(8,128)}) fusion(bf16[4096,896]{1,0:T(8,128)(2,1)} %param.12, bf16[2,896,4864]{2,1,0:T(8,128)(2,1)} %param.14), kind=kOutput, calls=%fused_computation.16 | convolution fusion | flops 35801530368 | bytes 135593984 | tf_op jit(solution)/shard_map/td,df->tf/dot_general | solution.py:22
  66.6 49.3 %fusion.33 = bf16[4096,896]{1,0:T(8,128)(2,1)} fusion(bf16[4096,4864]{1,0:T(8,128)(2,1)} %get-tuple-element.57, bf16[2,4864,896]{2,1,0:T(8,128)(2,1)} %param.15), kind=kOutput, calls=%fused_computation.37 | convolution fusion | flops 35705585664 | bytes 55902208 | tf_op jit(solution)/shard_map/tf,fd->td/dot_general | solution.py:25
  115.9 50.9 %fusion.17 = f32[4096,4864]{1,0:T(8,128)} fusion(bf16[4096,896]{1,0:T(8,128)(2,1)} %fusion.33, bf16[2,896,4864]{2,1,0:T(8,128)(2,1)} %param.14), kind=kOutput, calls=%fused_computation.23 | convolution fusion | flops 35701915648 | bytes 95748096 | tf_op jit(solution)/shard_map/td,df->tf/dot_general | solution.py:26
  166.8 67.9 %fusion.5 = bf16[4096,4864]{1,0:T(8,128)(2,1)} fusion(f32[4096,4864]{1,0:T(8,128)} %fusion.17, bf16[4096,896]{1,0:T(8,128)(2,1)} %param.13, bf16[2,4864,896]{2,1,0:T(8,128)(2,1)S(1)} %bitcast.67), kind=kOutput, calls=%fused_computation.7 | convolution fusion | flops 35901145088 | bytes 135593984 | tf_op jit(solution)/shard_map/td,fd->tf/dot_general | solution.py:30
  234.7 46.4 %fusion.43 = f32[896,4864]{1,0:T(8,128)} fusion(bf16[4096,896]{1,0:T(8,128)(2,1)} %fusion.33, bf16[4096,4864]{1,0:T(8,128)(2,1)} %fusion.5), kind=kOutput, calls=%fused_computation.67 | convolution fusion | flops 35701915648 | bytes 64618496
  281.1 0.0 reduce-scatter.15.cloned.1.call-update
  281.1 0.0 reduce-scatter.13.cloned.1.call-start
  281.2 49.5 %fusion.36 = bf16[4096,896]{1,0:T(8,128)(2,1)} fusion(bf16[4096,4864]{1,0:T(8,128)(2,1)} %fusion.5, bf16[2,896,4864]{2,1,0:T(8,128)(2,1)} %param.14), kind=kOutput, calls=%fused_computation.38 | convolution fusion | flops 35705585664 | bytes 55902208 | tf_op jit(solution)/shard_map/tf,df->td/dot_general | solution.py:32
  330.7 68.1 %fusion.11.clone.6 = bf16[4096,4864]{1,0:T(8,128)(2,1)} fusion(f32[4096,4864]{1,0:T(8,128)} %get-tuple-element.58, bf16[4096,896]{1,0:T(8,128)(2,1)} %fusion.36, bf16[2,4864,896]{2,1,0:T(8,128)(2,1)} %param.15), kind=kOutput, calls=%fused_computation.13.clone.clone.clone.clone.clone.1 | convolution fusion | flops 35901145088 | bytes 135593984 | tf_op jit(solution)/shard_map/td,fd->tf/dot_general | solution.py:34
  398.8 53.0 %fusion.14 = f32[896,4864]{0,1:T(8,128)} fusion(bf16[4096,896]{1,0:T(8,128)(2,1)} %param.12, bf16[4096,4864]{1,0:T(8,128)(2,1)} %fusion.11.clone.6), kind=kOutput, calls=%fused_computation.20 | convolution fusion | flops 35701915648 | bytes 64618496 | tf_op jit(solution)/shard_map/td,tf->df/dot_general | solution.py:35
  451.8 19.0 %copy.57 = f32[896,4864]{1,0:T(8,128)} copy(f32[896,4864]{0,1:T(8,128)} %fusion.14) | data formatting | bytes 34865152
  470.8 0.0 reduce-scatter.13.cloned.1.call-update
  470.8 0.0 reduce-scatter.9.cloned.1.call-start
  470.9 53.2 %fusion.44 = f32[4864,896]{1,0:T(8,128)} fusion(bf16[4096,4864]{1,0:T(8,128)(2,1)} %get-tuple-element.57, bf16[4096,896]{1,0:T(8,128)(2,1)} %fusion.36), kind=kOutput, calls=%fused_computation.68 | convolution fusion | flops 35701915648 | bytes 64618496 | tf_op jit(solution)/shard_map/tf,td->fd/dot_general | solution.py:33
  524.1 0.0 reduce-scatter.9.cloned.1.call-update
  524.1 0.0 reduce-scatter.11.cloned.1.call-start
  524.2 50.9 %fusion.12 = f32[4864,896]{1,0:T(8,128)} fusion(bf16[4096,896]{1,0:T(8,128)(2,1)} %param.13, f32[4096,4864]{1,0:T(8,128)} %fusion.17), kind=kOutput, calls=%fused_computation.18 | convolution fusion | flops 35801530368 | bytes 104464384 | tf_op jit(solution)/shard_map/tf,td->fd/dot_general | solution.py:29
  575.1 0.0 reduce-scatter.11.cloned.1.call-update
  575.1 0.0 all-gather.5.cloned.1.call-start
  575.1 0.0 reduce-scatter.15.cloned.1.call-done
  575.2 1.3 multiply_bitcast_fusion.2
  576.5 81.2 %reduce-scatter.13.cloned.1.call-done = f32[56,4864]{1,0:T(8,128)} async-done(((f32[896,4864]{1,0:T(8,128)}), f32[56,4864]{1,0:T(8,128)}) %reduce-scatter.13.cloned.1.call-update) | async-done | bytes 1089552 | tf_op jit(solution)/shard_map/reduce_scatter | solution.py:59
  657.7 1.3 multiply_bitcast_fusion.3
  659.0 1.2 multiply_reduce_fusion.5
  660.2 182.0 %reduce-scatter.9.cloned.1.call-done = f32[304,896]{1,0:T(8,128)} async-done(((f32[4864,896]{1,0:T(8,128)}), f32[304,896]{1,0:T(8,128)}) %reduce-scatter.9.cloned.1.call-update) | async-done | bytes 1089552 | tf_op jit(solution)/shard_map/reduce_scatter | solution.py:59
  842.1 1.3 multiply_bitcast_fusion.1
  843.5 183.5 %reduce-scatter.11.cloned.1.call-done = f32[304,896]{1,0:T(8,128)} async-done(((f32[4864,896]{1,0:T(8,128)}), f32[304,896]{1,0:T(8,128)}) %reduce-scatter.11.cloned.1.call-update) | async-done | bytes 1089552 | tf_op jit(solution)/shard_map/reduce_scatter | solution.py:59
  1027.0 1.3 multiply_bitcast_fusion
  1028.3 1.0 copy-done.1
  1029.3 1.2 multiply_reduce_fusion.4
  1032.4 30.9 %psum.14 = f32[]{:T(128)} all-reduce(f32[]{:T(128)S(6)} %add.58), channel_id=1, replica_groups=mesh['data'=16] {'data'}, use_global_device_ids=true, to_apply=%region_8.0 | all-reduce | flops 1 | bytes 8 | tf_op jit(solution)/shard_map/psum | solution.py:70
  1064.1 7.0 multiply_reduce_fusion
  1071.2 3.7 multiply_reduce_fusion.1
  1074.8 0.1 pad_maximum_fusion.2
  1075.7 32.7 %psum.15 = f32[8]{0:T(128)S(1)} all-reduce(f32[8]{0:T(128)S(1)} %pad_maximum_fusion.2), channel_id=1, replica_groups=mesh['data'=16] {'data'}, use_global_device_ids=true, to_apply=%region_11.0 | all-reduce | flops 8 | bytes 64 | tf_op jit(solution)/shard_map/psum | solution.py:75
  1108.4 0.1 rsqrt_multiply_fusion
  1108.5 0.1 slice_multiply_fusion
  1108.5 5.7 fusion.41
  1114.2 0.0 all-gather.5.cloned.1.call-update
  1114.2 0.3 all-gather.3.cloned.1.call-start
  1114.5 4.7 fusion.42
  1119.2 1.8 copy.54
  1121.0 0.0 all-gather.3.cloned.1.call-update
  1121.0 72.4 %all-gather.5.cloned.1.call-done = bf16[2,4864,896]{2,1,0:T(8,128)(2,1)} async-done(((bf16[2,304,896]{2,1,0:T(8,128)(2,1)}), bf16[2,4864,896]{2,1,0:T(8,128)(2,1)}) %all-gather.5.cloned.1.call-update) | async-done | bytes 17432592 | tf_op jit(solution)/shard_map/all_gather | solution.py:80
  1193.5 80.8 %all-gather.3.cloned.1.call-done = bf16[2,896,4864]{2,0,1:T(2,128)(2,1)} async-done(((bf16[2,56,4864]{2,0,1:T(2,128)(2,1)}), bf16[2,896,4864]{2,0,1:T(2,128)(2,1)}) %all-gather.3.cloned.1.call-update) | async-done | bytes 17432592 | tf_op jit(solution)/shard_map/all_gather | solution.py:79
  1274.3 16.7 %copy.55 = bf16[2,896,4864]{2,1,0:T(8,128)(2,1)} copy(bf16[2,896,4864]{2,0,1:T(2,128)(2,1)} %all-gather.3.cloned.1.call-done) | data formatting | bytes 34865152
  1291.0 6.4 copy.64
  (22 shorter events, 0.0 us)
Async XLA Ops:
  7.2 568.0 %reduce-scatter.15.cloned.1.call-start = ((), (), s32[]{:S(2)}) async-start(), calls=%async_computation.9 | async-start | bytes 18522112 | tf_op jit(solution)/shard_map/reduce_scatter | solution.py:59
  66.6 100.2 %slice-start = ((s8[17432576]{0:T(1024)(128)(4,1)}), s8[655360]{0:T(1024)(128)(4,1)S(1)}, s32[]{:S(2)}) async-start(s8[17432576]{0:T(1024)(128)(4,1)} %bitcast.66), calls=%async_computation.10 | async-start | bytes 1310720
  66.6 100.2 %slice-start.1 = ((s8[17432576]{0:T(1024)(128)(4,1)}), s8[4194304]{0:T(1024)(128)(4,1)S(1)}, s32[]{:S(2)}) async-start(s8[17432576]{0:T(1024)(128)(4,1)} %bitcast.66), calls=%async_computation.11 | async-start | bytes 8388608
  66.6 100.2 %slice-start.2 = ((s8[17432576]{0:T(1024)(128)(4,1)}), s8[4194304]{0:T(1024)(128)(4,1)S(1)}, s32[]{:S(2)}) async-start(s8[17432576]{0:T(1024)(128)(4,1)} %bitcast.66), calls=%async_computation.12 | async-start | bytes 8388608
  115.9 50.9 %slice-start.3 = ((s8[17432576]{0:T(1024)(128)(4,1)}), s8[4194304]{0:T(1024)(128)(4,1)S(1)}, s32[]{:S(2)}) async-start(s8[17432576]{0:T(1024)(128)(4,1)} %bitcast.66), calls=%async_computation.13 | async-start | bytes 8388608
  115.9 50.9 %slice-start.4 = ((s8[17432576]{0:T(1024)(128)(4,1)}), s8[4194304]{0:T(1024)(128)(4,1)S(1)}, s32[]{:S(2)}) async-start(s8[17432576]{0:T(1024)(128)(4,1)} %bitcast.66), calls=%async_computation.14 | async-start | bytes 8388608
  281.1 376.6 %reduce-scatter.13.cloned.1.call-start = ((), (), s32[]{:S(2)}) async-start(), calls=%async_computation.8 | async-start | bytes 18522112 | tf_op jit(solution)/shard_map/reduce_scatter | solution.py:59
  470.8 371.3 %reduce-scatter.9.cloned.1.call-start = ((), (), s32[]{:S(2)}) async-start(), calls=%async_computation.4 | async-start | bytes 18522112 | tf_op jit(solution)/shard_map/reduce_scatter | solution.py:59
  524.1 502.9 %reduce-scatter.11.cloned.1.call-start = ((), (), s32[]{:S(2)}) async-start(), calls=%async_computation.5 | async-start | bytes 18522112 | tf_op jit(solution)/shard_map/reduce_scatter | solution.py:59
  575.1 618.4 %all-gather.5.cloned.1.call-start = ((), (), s32[]{:S(2)}) async-start(), calls=%async_computation.7 | async-start | bytes 18522112 | tf_op jit(solution)/shard_map/all_gather | solution.py:80
  1028.3 1.0 copy-start.1
  1064.1 7.1 copy-start.2
  1064.1 7.1 copy-start.4
  1064.1 7.1 copy-start.5
  1074.8 39.7 %copy-start.3 = (f32[2,56,4864]{2,1,0:T(8,128)S(1)}, f32[2,56,4864]{2,1,0:T(8,128)}, u32[]{:S(2)}) copy-start(f32[2,56,4864]{2,1,0:T(8,128)} %param.16) | copy-start | bytes 6537220
  1114.2 160.1 %all-gather.3.cloned.1.call-start = ((), (), s32[]{:S(2)}) async-start(), calls=%async_computation.6 | async-start | bytes 18522112 | tf_op jit(solution)/shard_map/all_gather | solution.py:79
  1274.3 16.7 %copy-start = (bf16[2,4864,896]{2,1,0:T(8,128)(2,1)S(1)}, bf16[2,4864,896]{2,1,0:T(8,128)(2,1)}, u32[]{:S(2)}) copy-start(bf16[2,4864,896]{2,1,0:T(8,128)(2,1)} %all-gather.5.cloned.1.call-done) | copy-start | bytes 52297732
Sparse Core Ops, SparseCore 0:
  281.3 186.7 reduce-scatter.14
  470.9 186.7 reduce-scatter.12
  660.0 182.0 reduce-scatter.8
  844.9 182.0 reduce-scatter.10
  1114.4 79.0 all-gather.4
  1196.1 78.1 all-gather.2
where the time goes:
time: 1310 us
  waiting for transfers between devices  600 us (46%)
  matrix products  549 us (42%)
  blocking collectives  63.6 us (5%)
  local copies, waits for them, and re-layouts  44.9 us (3%)
  other arithmetic  28.8 us (2%)
  between operations  19.3 us (1%)
    reduce_scatter x4, waiting for transfers between devices, reduce_rows(): lax.psum_scatter(grad, 'data', scatter_dimension=0, tiled=True) / group_size  447 us
    all_gather x1, waiting for transfers between devices, device_step(): lax.all_gather(master_up_out.astype(jnp.bfloat16), 'data', axis=1, tiled=...  80.8 us
    all_gather x1, waiting for transfers between devices, device_step(): lax.all_gather(master_down_out.astype(jnp.bfloat16), 'data', axis=1, tile...  72.4 us
    dot_general x1, matrix products, local_grads(): jnp.einsum('td,fd->tf', d_hidden, w_down[0], preferred_element_type=jnp.f...  68.1 us
    dot_general x1, matrix products, local_grads(): jnp.einsum('td,fd->tf', grad_out, w_down[1], preferred_element_type=jnp.f...  67.9 us
    dot_general x1, matrix products, local_grads(): jnp.einsum('td,df->tf', act_in, w_up[0], preferred_element_type=jnp.float32)  59.4 us
    dot_general x1, matrix products, local_grads(): jnp.einsum('tf,td->fd', act_one, d_hidden, preferred_element_type=jnp.flo...  53.2 us
    dot_general x1, matrix products, local_grads(): jnp.einsum('td,tf->df', act_in, dz_one, preferred_element_type=jnp.float32)  53 us
  transfers between devices with their start and end apart: 6, of which 5 were waited for; matrix products, arithmetic and copies ran while one was open for 23% of the time, Pallas kernels for 0%

commit v1 on v0

v1 whole, which is shorter than its diff:
```python
import functools

import jax
import jax.numpy as jnp
from jax import lax
from jax.experimental import pallas as pl
from jax.experimental.pallas import tpu as pltpu
from jax.sharding import PartitionSpec as P

STEP = 10
BETA_ONE = 0.9
BETA_TWO = 0.95
ADAM_EPS = 1e-8
NORM_EPS = 1e-6
INV_SQRT_TWO = 0.7071067811865476
INV_SQRT_TWO_PI = 0.3989422804014327

GROUP = 16
TOKENS = 4096
D = 896
FF = 4864
TILE = 256
STEPS = FF // TILE
UP_ROWS = D // GROUP
DOWN_ROWS = FF // GROUP
DOWN_UNIT = DOWN_ROWS // STEPS
LAG = 2
DRAIN = 1 + 3 * LAG
SLOTS = LAG + 3
SUM_SLOTS = 3 * LAG
BLOCK = 512
MESH = pl.DeviceIdType.MESH
F32 = jnp.float32
BF16 = jnp.bfloat16


def gelu_parts(pre_act):
    normal_cdf = 0.5 * (1.0 + lax.erf(pre_act * INV_SQRT_TWO))
    normal_pdf = jnp.exp(-0.5 * pre_act * pre_act) * INV_SQRT_TWO_PI
    return pre_act * normal_cdf, normal_cdf + pre_act * normal_pdf


def dot_last(left, right):
    return lax.dot_general(left, right, (((1,), (1,)), ((), ())), preferred_element_type=F32)


def greet(devices):
    barrier = pltpu.get_barrier_semaphore()
    for device in devices:
        pl.semaphore_signal(barrier, inc=1, device_id=(device,), device_id_type=MESH)
    pl.semaphore_wait(barrier, len(devices))


class ReduceScatter:
    def __init__(self, phase, gbuf, rc, sums, r1, r2, r3, send, recv):
        self.phase = phase
        self.gbuf, self.rc, self.sums, self.landed = gbuf, rc, sums, (r1, r2, r3)
        self.send, self.recv = send, recv
        self.me = lax.axis_index("data")
        self.core = lax.rem(self.me, 2)
        self.chip = self.me // 2

    def stride_bit(self, unit, stage):
        axis = lax.rem(unit + self.phase + (0, 2, 1)[stage - 1], 3)
        stride = 1 + axis + axis * (axis - 1) // 2
        return stride, lax.rem(self.chip // stride, 2)

    def copy(self, stage, unit):
        if stage == 0:
            slot = lax.rem(unit, 2)
            src, dst = self.gbuf.at[slot, :, 1 - self.core], self.rc.at[slot]
            device = self.me + 1 - 2 * self.core
        else:
            slot = lax.rem(unit, SLOTS)
            count = 8 >> stage
            src = self.sums.at[lax.rem(unit, SUM_SLOTS), pl.ds(count, count)]
            dst = self.landed[stage - 1].at[slot]
            stride, bit = self.stride_bit(unit, stage)
            device = self.me + 2 * stride * (1 - 2 * bit)
        return pltpu.make_async_remote_copy(src_ref=src, dst_ref=dst, send_sem=self.send.at[stage, slot], recv_sem=self.recv.at[stage, slot], device_id=(device,), device_id_type=MESH)

    def finish(self, stage, unit):
        self.copy(stage, unit).wait()
        held = lax.rem(unit, SUM_SLOTS)
        if stage == 0:
            slot = lax.rem(unit, 2)
            parts = [self.stride_bit(unit, s) for s in (1, 2, 3)]
            for pos in range(8):
                chip = 0
                for (stride, bit), flip in zip(parts, (pos // 4, pos // 2 % 2, pos % 2)):
                    chip = chip + (1 - bit if flip else bit) * stride
                self.sums[held, pos] = self.gbuf[slot, chip, self.core] + self.rc[slot, chip]
        elif stage < 3:
            count = 8 >> stage
            slot = lax.rem(unit, SLOTS)
            for pos in range(count):
                self.sums[held, pos] = self.sums[held, pos] + self.landed[stage - 1][slot, pos]
        else:
            return self.sums[held, 0] + self.landed[2][lax.rem(unit, SLOTS), 0]


def within(unit):
    return jnp.logical_and(unit >= 0, unit < STEPS)


def backward_kernel(has_dx, *refs):
    if has_dx:
        z_ref, dy_ref, wd_ref, left_ref, gd_ref, wu_ref, up_ref, down_ref, dx_ref = refs[:9]
        qbuf, acc, stage_buf = refs[9:12]
        rest = refs[12:]
    else:
        z_ref, dy_ref, wd_ref, left_ref, gd_ref, up_ref, down_ref = refs[:7]
        qbuf = refs[7]
        rest = refs[8:]
    up = ReduceScatter(0, *rest[0:8])
    down = ReduceScatter(1, *rest[8:16])
    load_sem, out_sem = rest[16:18]
    step = pl.program_id(0)

    def load(unit):
        slot = lax.rem(unit, 2)
        return pltpu.make_async_copy(gd_ref.at[:, :, pl.ds(pl.multiple_of(unit * DOWN_UNIT, DOWN_UNIT), DOWN_UNIT)], down.gbuf.at[slot], load_sem.at[slot])

    @pl.when(step == 0)
    def _():
        me, core, chip = up.me, up.core, up.chip
        greet([me + 1 - 2 * core] + [me + 2 * s * (1 - 2 * lax.rem(chip // s, 2)) for s in (1, 2, 4)])
        load(0).start()
        if has_dx:
            acc[...] = jnp.zeros_like(acc)

    @pl.when(step < STEPS)
    def _():
        def block(index, carry):
            rows = pl.ds(pl.multiple_of(index * BLOCK, BLOCK), BLOCK)
            slope = gelu_parts(z_ref[rows, :])[1]
            grad = (dot_last(dy_ref[rows, :], wd_ref[...]) * slope).astype(BF16)
            qbuf[rows, :] = grad
            if has_dx:
                acc[rows, :] += dot_last(grad, wu_ref[...])
            return carry

        lax.fori_loop(0, TOKENS // BLOCK, block, 0)
        tile = jnp.dot(left_ref[...], qbuf[...], preferred_element_type=F32)
        slot = lax.rem(step, 2)
        for i in range(GROUP):
            up.gbuf[slot, i // 2, i % 2] = tile[i * UP_ROWS:(i + 1) * UP_ROWS, :]

    @pl.when(within(step - DRAIN))
    def _():
        unit = step - DRAIN
        up_ref[:, pl.ds(pl.multiple_of(unit * TILE, TILE), TILE)] = up.finish(3, unit)
        down_ref[pl.ds(pl.multiple_of(unit * DOWN_UNIT, DOWN_UNIT), DOWN_UNIT), :] = down.finish(3, unit)

    for stage in (2, 1, 0):
        unit = step - 1 - stage * LAG

        @pl.when(within(unit))
        def _():
            for ring in (up, down):
                ring.finish(stage, unit)
                ring.copy(stage + 1, unit).start()

    @pl.when(step < STEPS - 1)
    def _():
        load(step + 1).start()

    @pl.when(step < STEPS)
    def _():
        up.copy(0, step).start()
        load(step).wait()
        down.copy(0, step).start()

    if has_dx:
        @pl.when(step == STEPS - 1)
        def _():
            def flush(index, carry):
                rows = pl.ds(pl.multiple_of(index * BLOCK, BLOCK), BLOCK)
                stage_buf[...] = acc[rows, :].astype(BF16)
                out = pltpu.make_async_copy(stage_buf, dx_ref.at[rows, :], out_sem)
                out.start()
                out.wait()
                return carry

            lax.fori_loop(0, TOKENS // BLOCK, flush, 0)


def ring_scratch(rows, columns):
    block = (rows, columns)
    return [
        pltpu.VMEM((2, 8, 2) + block, F32),
        pltpu.VMEM((2, 8) + block, F32),
        pltpu.VMEM((SUM_SLOTS, 8) + block, F32),
        pltpu.VMEM((SLOTS, 4) + block, F32),
        pltpu.VMEM((SLOTS, 2) + block, F32),
        pltpu.VMEM((SLOTS, 1) + block, F32),
        pltpu.SemaphoreType.DMA((4, SLOTS)),
        pltpu.SemaphoreType.DMA((4, SLOTS)),
    ]


def backward_block(pre_act, grad, w_down, left, grad_down, w_up, collective_id):
    has_dx = w_up is not None
    last = STEPS - 1
    whole = pl.Buffered(buffer_count=1)
    in_specs = [
        pl.BlockSpec((TOKENS, TILE), lambda s: (0, jnp.minimum(s, last))),
        pl.BlockSpec((TOKENS, D), lambda s: (0, 0), pipeline_mode=whole),
        pl.BlockSpec((TILE, D), lambda s: (jnp.minimum(s, last), 0)),
        pl.BlockSpec((D, TOKENS), lambda s: (0, 0), pipeline_mode=whole),
        pl.BlockSpec(memory_space=pl.ANY),
    ]
    args = [pre_act, grad, w_down, left, grad_down.reshape(8, 2, DOWN_ROWS, D)]
    out_shape = [jax.ShapeDtypeStruct((UP_ROWS, FF), F32), jax.ShapeDtypeStruct((DOWN_ROWS, D), F32)]
    out_specs = [pl.BlockSpec((UP_ROWS, FF), lambda s: (0, 0)), pl.BlockSpec((DOWN_ROWS, D), lambda s: (0, 0))]
    scratch = [pltpu.VMEM((TOKENS, TILE), BF16)]
    if has_dx:
        in_specs.append(pl.BlockSpec((D, TILE), lambda s: (0, jnp.minimum(s, last))))
        args.append(w_up)
        out_shape.append(jax.ShapeDtypeStruct((TOKENS, D), BF16))
        out_specs.append(pl.BlockSpec(memory_space=pl.ANY))
        scratch += [pltpu.VMEM((TOKENS, D), F32), pltpu.VMEM((BLOCK, D), BF16)]
    scratch += ring_scratch(UP_ROWS, TILE) + ring_scratch(DOWN_UNIT, D)
    scratch += [pltpu.SemaphoreType.DMA((2,)), pltpu.SemaphoreType.DMA]
    return pl.pallas_call(
        functools.partial(backward_kernel, has_dx),
        grid=(STEPS + DRAIN,),
        in_specs=in_specs,
        out_specs=out_specs,
        out_shape=out_shape,
        scratch_shapes=scratch,
        compiler_params=pltpu.CompilerParams(collective_id=collective_id, has_side_effects=True, vmem_limit_bytes=67043328, dimension_semantics=("arbitrary",)),
        cost_estimate=pl.CostEstimate(flops=(6 if has_dx else 4) * TOKENS * D * FF, bytes_accessed=150 * 2**20, transcendentals=2 * TOKENS * FF),
    )(*args)


COLUMN_PARTS = ((0, 1664), (1664, 1664), (3328, 1536))
ROW_PARTS = ((0, 112), (112, 96), (208, 96))
ORDERS = ((2, 1, 0), (1, 0, 2), (0, 2, 1))
CHUNKS = 12


def tail_kernel(scalars, g1, g2, g3, g4, master_up, master_down, avg_up, avg_down, sq_up, sq_down, w_up_out, w_down_out, master_up_out, master_down_out, avg_up_out, avg_down_out, sq_up_out, sq_down_out, norm_out, send_up, send_down, dir_up, dir_down, mine, stats, stat_send, stat_recv, send_sem, recv_sem, own_sem):
    me = lax.axis_index("data")
    core = lax.rem(me, 2)
    coords = (me // 8, lax.rem(me // 4, 2), lax.rem(me // 2, 2))
    sibling = me + 1 - 2 * core
    others = [lax.rem(me + k, GROUP) for k in range(1, GROUP)]
    greet(others)

    def share(turn, row):
        mine[turn] = row
        copies = []
        for k, device in enumerate(others):
            copies.append(pltpu.make_async_remote_copy(src_ref=mine.at[turn], dst_ref=stats.at[turn, me], send_sem=stat_send.at[turn, k], recv_sem=stat_recv.at[turn, me], device_id=(device,), device_id_type=MESH))
            copies[-1].start()
        stats[turn, me] = row
        for k, device in enumerate(others):
            copies[k].wait_send()
            pltpu.make_async_remote_copy(src_ref=mine.at[turn], dst_ref=stats.at[turn, device], send_sem=stat_send.at[turn, k], recv_sem=stat_recv.at[turn, device], device_id=(device,), device_id_type=MESH).wait_recv()
        return jnp.sum(stats[turn], axis=0)

    def sum_square(values):
        return jnp.sum(values * values)

    grads = ((g1, g3), (g2, g4))
    scale = 1.0 / GROUP
    local = sum_square(g1[...] * scale) + sum_square(g3[...] * scale) + sum_square(g2[...] * scale) + sum_square(g4[...] * scale)
    total = share(0, jnp.full((8, 128), local, F32))
    norm = jnp.sqrt(total)
    clip = jnp.minimum(1.0, scalars[1] / (norm + NORM_EPS))
    norm_out[...] = norm
    clip = clip[0:1, 0:1]
    bias_one = 1.0 - BETA_ONE ** STEP
    bias_two = 1.0 - BETA_TWO ** STEP
    lane = lax.broadcasted_iota(jnp.int32, (8, 128), 1)
    row = jnp.zeros((8, 128), F32)
    families = ((master_up, avg_up, sq_up, avg_up_out, sq_up_out, dir_up), (master_down, avg_down, sq_down, avg_down_out, sq_down_out, dir_down))
    for f, (master, avg, sq, avg_out, sq_out, direction) in enumerate(families):
        for k in range(2):
            g = grads[f][k][...] * scale
            avg_new = BETA_ONE * avg[k] + (1.0 - BETA_ONE) * clip * g
            sq_new = BETA_TWO * sq[k] + (1.0 - BETA_TWO) * (clip * clip) * (g * g)
            u = (avg_new / bias_one) / (jnp.sqrt(sq_new / bias_two) + ADAM_EPS)
            avg_out[k] = avg_new
            sq_out[k] = sq_new
            direction[k] = u
            row = row + jnp.where(lane == 2 * f + k, sum_square(master[k]), 0.0) + jnp.where(lane == 4 + 2 * f + k, sum_square(u), 0.0)
    totals = share(1, row)

    def out_view(chunk, picks, flipped=None):
        index = []
        for axis in range(3):
            if axis in picks:
                index.append(slice(None))
            elif axis == flipped:
                index.append(1 - coords[axis])
            else:
                index.append(coords[axis])
        family, k, (start, size) = chunk
        if family == 0:
            return w_up_out.at[(k, *index, core, slice(None), pl.ds(start, size))]
        return w_down_out.at[(k, *index, core, pl.ds(start, size), slice(None))]

    def neighbour(axis):
        stride = (8, 4, 2)[axis]
        return me + stride * (1 - 2 * coords[axis])

    def remote(n, kind, src, dst, device):
        return pltpu.make_async_remote_copy(src_ref=src, dst_ref=dst, send_sem=send_sem.at[n, kind], recv_sem=recv_sem.at[n, kind], device_id=(device,), device_id_type=MESH)

    chunks = []
    for f, parts in enumerate((COLUMN_PARTS, ROW_PARTS)):
        for k in range(2):
            chunks += [(f, k, part) for part in parts]
    order = [ORDERS[n % 3] for n in range(CHUNKS)]
    pending = []
    rounds = [[], [], []]
    locals_ = []
    for f, (master, master_out, direction, send) in enumerate(((master_up, master_up_out, dir_up, send_up), (master_down, master_down_out, dir_down, send_down))):
        for k in range(2):
            i = 2 * f + k
            ratio = jnp.sqrt(totals[0:1, i:i + 1]) / jnp.sqrt(totals[0:1, 4 + i:5 + i])
            new = master[k] - scalars[0] * ratio * direction[k]
            master_out[k] = new
            send[k] = new.astype(BF16)
            for part in range(3):
                n = 3 * i + part
                start, size = chunks[n][2]
                if f == 0:
                    src = send.at[k, :, pl.ds(start, size)]
                else:
                    src = send.at[k, pl.ds(start, size), :]
                dst = out_view(chunks[n], ())
                rounds[0].append(remote(n, 0, src, dst, neighbour(order[n][0])))
                rounds[0][-1].start()
                pending.append(remote(n, 3, src, dst, sibling))
                pending[-1].start()
                locals_.append(pltpu.make_async_copy(src, dst, own_sem.at[n]))
                locals_[-1].start()
    for turn in range(3):
        for n in range(CHUNKS):
            first, second, third = order[n]
            if turn == 0:
                locals_[n].wait()
            rounds[turn][n].wait()
            gathered = order[n][:turn]
            view = out_view(chunks[n], gathered, order[n][turn])
            pending.append(remote(n, 4 + turn, view, view, sibling))
            pending[-1].start()
            if turn < 2:
                view = out_view(chunks[n], order[n][:turn + 1])
                rounds[turn + 1].append(remote(n, turn + 1, view, view, neighbour(order[n][turn + 1])))
                rounds[turn + 1][-1].start()
    for copy in pending:
        copy.wait()


def tail(scalars, grads, states):
    vmem = pl.BlockSpec(memory_space=pltpu.VMEM)
    any_space = pl.BlockSpec(memory_space=pl.ANY)
    up, down = (2, UP_ROWS, FF), (2, DOWN_ROWS, D)
    shape = jax.ShapeDtypeStruct
    return pl.pallas_call(
        tail_kernel,
        in_specs=[pl.BlockSpec(memory_space=pltpu.SMEM)] + [vmem] * 10,
        out_specs=[any_space] * 2 + [vmem] * 7,
        out_shape=[
            shape((2, 2, 2, 2, 2, UP_ROWS, FF), BF16),
            shape((2, 2, 2, 2, 2, DOWN_ROWS, D), BF16),
            shape(up, F32), shape(down, F32), shape(up, F32), shape(down, F32), shape(up, F32), shape(down, F32),
            shape((8, 128), F32),
        ],
        scratch_shapes=[
            pltpu.VMEM(up, BF16), pltpu.VMEM(down, BF16), pltpu.VMEM(up, F32), pltpu.VMEM(down, F32),
            pltpu.VMEM((2, 8, 128), F32), pltpu.VMEM((2, GROUP, 8, 128), F32),
            pltpu.SemaphoreType.DMA((2, GROUP)), pltpu.SemaphoreType.DMA((2, GROUP)),
            pltpu.SemaphoreType.DMA((CHUNKS, 7)), pltpu.SemaphoreType.DMA((CHUNKS, 7)), pltpu.SemaphoreType.DMA((CHUNKS,)),
        ],
        compiler_params=pltpu.CompilerParams(collective_id=3, has_side_effects=True, vmem_limit_bytes=67043328),
    )(scalars, *grads, *states)


def solution(mesh):
    batch_rows = P("data", None)
    state_rows = P(None, "data", None)
    replicated = P()

    def device_step(act_in, grad_out, w_up, w_down, master_up, master_down, exp_avg_up, exp_avg_down, exp_sq_up, exp_sq_down, learn_rate, clip_norm):
        z_one = jnp.dot(act_in, w_up[0], preferred_element_type=F32)
        act_one = gelu_parts(z_one)[0].astype(BF16)
        hidden = jnp.dot(act_one, w_down[0], preferred_element_type=F32).astype(BF16)
        z_three = jnp.dot(hidden, w_up[1], preferred_element_type=F32)
        act_three = gelu_parts(z_three)[0].astype(BF16)
        g_four = jnp.dot(act_three.T, grad_out, preferred_element_type=F32)
        shard_three, shard_four, d_hidden = backward_block(z_three, grad_out, w_down[1], hidden.T, g_four, w_up[1], 1)
        g_two = jnp.dot(act_one.T, d_hidden, preferred_element_type=F32)
        shard_one, shard_two = backward_block(z_one, d_hidden, w_down[0], act_in.T, g_two, None, 2)
        scalars = jnp.stack([learn_rate, clip_norm])
        outs = tail(scalars, (shard_one, shard_two, shard_three, shard_four), (master_up, master_down, exp_avg_up, exp_avg_down, exp_sq_up, exp_sq_down))
        new_w_up = outs[0].reshape(2, D, FF)
        new_w_down = outs[1].reshape(2, FF, D)
        return (new_w_up, new_w_down, *outs[2:8], outs[8][0, 0])

    return jax.shard_map(device_step, mesh=mesh, in_specs=(batch_rows, batch_rows, replicated, replicated, state_rows, state_rows, state_rows, state_rows, state_rows, state_rows, replicated, replicated), out_specs=(replicated, replicated, state_rows, state_rows, state_rows, state_rows, state_rows, state_rows, replicated), check_vma=False)
```

time: 1310 us -> 925 us (0.71)
  waiting for transfers between devices: 600 us -> 0 us
  Pallas kernels: 0 us -> 590 us
  matrix products: 549 us -> 266 us
  blocking collectives: 63.6 us -> 0 us
  other arithmetic: 28.8 us -> 0.59 us
  between operations: 19.3 us -> 2.47 us
  local copies, waits for them, and re-layouts: 44.9 us -> 58.5 us
    pallas_call x0 -> x3, Pallas kernels: none -> 590 us  [the longest x2 442 us: backward_block(): pl.pallas_call(functools.partial(backward_kernel, has_dx), grid=(STEPS +...]
    reduce_scatter x4 -> x0, waiting for transfers between devices: 447 us -> none  [reduce_rows(): lax.psum_scatter(grad, 'data', scatter_dimension=0, tiled=True) / group_size]
    dot_general x9 -> x5, matrix products: 502 us -> 266 us  [the longest x1 62.1 us: device_step(): g_two = jnp.dot(act_one.T, d_hidden, preferred_element_type=F32)]
    all_gather x2 -> x0, waiting for transfers between devices: 153 us -> none  [the longest x1 80.8 us: device_step(): lax.all_gather(master_up_out.astype(jnp.bfloat16), 'data', axis=1, tiled=...]
    psum x2 -> x0, blocking collectives: 63.6 us -> none  [the longest x1 32.7 us: device_step(): norm_stats = lax.psum(local_stats, 'data')]
    unnamed x1 -> x0, matrix products: 46.4 us -> none
    squeeze x0 -> x2, local copies, waits for them, and re-layouts: none -> 14 us  [the longest x1 7.51 us: device_step(): z_three = jnp.dot(hidden, w_up[1], preferred_element_type=F32)]
    unnamed x25 -> x43, local copies, waits for them, and re-layouts: 43.1 us -> 43.3 us
  transfers between devices with their start and end apart: 6 -> 0, of which waited for: 5 -> 0; matrix products, arithmetic and copies ran while one was open for 23% -> 0% of each run, Pallas kernels for 0% -> 0%
where the time goes in v1:
time: 925 us; the launch traced here: 917 us
  Pallas kernels  590 us (64%)
  matrix products  266 us (29%)
  local copies, waits for them, and re-layouts  58.5 us (6%)
    pallas_call x2, Pallas kernels, backward_block(): pl.pallas_call(functools.partial(backward_kernel, has_dx), grid=(STEPS +...  442 us
    pallas_call x1, Pallas kernels, tail(): pl.pallas_call(tail_kernel, in_specs=[pl.BlockSpec(memory_space=pltpu.SME...  148 us
    dot_general x1, matrix products, device_step(): g_two = jnp.dot(act_one.T, d_hidden, preferred_element_type=F32)  62.1 us
    dot_general x1, matrix products, device_step(): z_one = jnp.dot(act_in, w_up[0], preferred_element_type=F32)  59.3 us
    dot_general x1, matrix products, device_step(): z_three = jnp.dot(hidden, w_up[1], preferred_element_type=F32)  51.1 us
    dot_general x1, matrix products, device_step(): g_four = jnp.dot(act_three.T, grad_out, preferred_element_type=F32)  49.7 us
    dot_general x1, matrix products, device_step(): jnp.dot(act_one, w_down[0], preferred_element_type=F32).astype(BF16)  43.6 us
    unnamed x43, local copies, waits for them, and re-layouts  43.3 us

profile of v1, /device:TPU:0, one launch (start us, length us, event | category | flops | bytes accessed | tf_op | source)
XLA Modules:
  0.0 917.2 jit_solution(12959114838026245985)
XLA Ops:
  0.6 59.3 %multiply_convert_fusion.1 = (bf16[4096,4864]{1,0:T(8,128)(2,1)}, f32[4096,4864]{1,0:T(8,128)}) fusion(bf16[4096,896]{1,0:T(8,128)(2,1)} %param.12, bf16[2,896,4864]{2,1,0:T(8,128)(2,1)} %param.14), kind=kOutput, calls=%fused_computation.1 | convolution fusion | flops 35801530368 | bytes 135593984 | tf_op jit(solution)/shard_map/dot_general | solution.py:390
  60.0 43.6 %convolution_convert_fusion = bf16[4096,896]{0,1:T(8,128)(2,1)} fusion(bf16[4096,4864]{1,0:T(8,128)(2,1)} %get-tuple-element.39, bf16[2,4864,896]{2,1,0:T(8,128)(2,1)} %param.15), kind=kOutput, calls=%fused_computation.9 | convolution fusion | flops 35705585664 | bytes 55902208 | tf_op jit(solution)/shard_map/dot_general | solution.py:392
  103.6 0.0 copy-start.6
  103.6 0.0 slice-start
  103.6 0.0 slice-start.1
  103.6 51.1 %fusion.7.refs_0_ = f32[4096,4864]{1,0:T(8,128)} fusion(bf16[4096,896]{0,1:T(8,128)(2,1)} %convolution_convert_fusion, bf16[2,896,4864]{2,1,0:T(8,128)(2,1)} %param.14), kind=kOutput, calls=%fused_computation.14 | convolution fusion | flops 35701915648 | bytes 95748096 | tf_op jit(solution)/shard_map/dot_general | solution.py:393
  154.8 0.0 copy-done.6
  154.8 0.0 slice-start.2
  154.8 0.0 slice-start.3
  154.8 0.0 slice-start.4
  154.8 49.7 %fusion = f32[4864,896]{1,0:T(8,128)} fusion(bf16[4096,896]{1,0:T(8,128)(2,1)S(1)} %copy-done.6, f32[4096,4864]{1,0:T(8,128)} %fusion.7.refs_0_), kind=kOutput, calls=%fused_computation.2 | convolution fusion | flops 35801530368 | bytes 104464384 | tf_op jit(solution)/shard_map/dot_general | solution.py:395
  204.4 0.0 slice-done
  204.4 0.0 slice-done.1
  204.4 0.0 slice-done.2
  204.4 0.0 slice-done.3
  204.5 0.0 slice-done.4
  204.5 6.5 slice_bitcast_fusion.2
  210.9 7.5 slice_bitcast_fusion.1.refs_5_
  218.4 281.1 %shard_map.187 = (f32[56,4864]{1,0:T(8,128)}, f32[304,896]{1,0:T(8,128)}, bf16[4096,896]{1,0:T(8,128)(2,1)}) custom-call(f32[4096,4864]{1,0:T(8,128)} %fusion.7.refs_0_, bf16[4096,896]{1,0:T(8,128)(2,1)} %refs_1_.1, bf16[4864,896]{1,0:T(8,128)(2,1)} %get-tuple-element.38.refs_2_, bf16[896,4096]{1,0:T(8,128)(2,1)} %bitcast.46, f32[8,2,304,896]{3,2,1,0:T(8,128)} %bitcast.44, ...), custom_call_target="tpu_custom_call" | custom-call | flops 107105746944 | bytes 157286400 | tf_op jit(solution)/shard_map/pallas_call | solution.py:225
  499.5 62.1 %fusion.8 = f32[4864,896]{1,0:T(8,128)} fusion(bf16[4096,4864]{1,0:T(8,128)(2,1)} %get-tuple-element.39, bf16[4096,896]{1,0:T(8,128)(2,1)} %get-tuple-element.23.refs_1_), kind=kOutput, calls=%fused_computation.15 | convolution fusion | flops 35701915648 | bytes 64618496 | tf_op jit(solution)/shard_map/dot_general | solution.py:397
  561.6 10.8 %copy.22 = bf16[4096,896]{0,1:T(8,128)(2,1)} copy(bf16[4096,896]{1,0:T(8,128)(2,1)} %param.12) | data formatting | bytes 14680064 | tf_op args[0]
  572.4 160.5 %shard_map.188 = (f32[56,4864]{1,0:T(8,128)}, f32[304,896]{1,0:T(8,128)}) custom-call(f32[4096,4864]{1,0:T(8,128)} %get-tuple-element.40.refs_0_, bf16[4096,896]{1,0:T(8,128)(2,1)} %get-tuple-element.23.refs_1_, bf16[4864,896]{1,0:T(8,128)(2,1)} %get-tuple-element.37.refs_2_, bf16[896,4096]{1,0:T(8,128)(2,1)} %bitcast.43, f32[8,2,304,896]{3,2,1,0:T(8,128)} %bitcast.45), custom_call_target="tpu_custom_call" | custom-call | flops 71403831296 | bytes 157286400 | tf_op jit(solution)/shard_map/pallas_call | solution.py:225
  734.2 0.6 pad_maximum_fusion.scalars
  734.8 148.2 %shard_map.189 = (bf16[2,2,2,2,2,56,4864]{6,5,4,3,2,1,0:T(8,128)(2,1)}, bf16[2,2,2,2,2,304,896]{6,5,4,3,2,1,0:T(8,128)(2,1)}, f32[2,56,4864]{2,1,0:T(8,128)}, f3...) custom-call(f32[2]{0:T(128)} %pad_maximum_fusion.scalars, ...), custom_call_target="tpu_custom_call" | custom-call | tf_op jit(solution)/shard_map/pallas_call | solution.py:364
  883.0 1.2 slice.21
  884.2 0.0 slice-start.5
  884.2 0.0 slice-start.9
  884.2 16.8 %copy.34 = bf16[2,896,4864]{2,1,0:T(8,128)(2,1)} copy(bf16[2,896,4864]{2,1,0:T(8,128)(2,1)} %bitcast.42) | data formatting | bytes 34865152
  901.0 0.0 slice-done.5
  901.0 0.0 slice-done.6
  901.0 0.0 slice-done.7
  901.0 0.0 slice-done.8
  901.0 0.0 slice-done.9
  901.0 0.0 copy-start.5
  901.0 0.0 copy-start.4
  901.0 7.3 copy.35
  908.3 0.0 copy-done.5
  908.4 1.3 copy.36
  909.7 0.0 copy-done.4
  909.7 1.3 copy.37
  911.1 0.0 copy-done.3
  911.1 1.3 copy.38
  912.4 0.2 copy-done.2
  912.6 1.3 copy.39
  913.9 0.0 copy-done.1
  913.9 1.3 copy.40
  915.3 0.1 copy-done
  915.4 1.3 copy.41
  (9 shorter events, 0.0 us)
Async XLA Ops:
  103.6 51.1 %copy-start.6 = (bf16[4096,896]{1,0:T(8,128)(2,1)S(1)}, bf16[4096,896]{1,0:T(8,128)(2,1)}, u32[]{:S(2)}) copy-start(bf16[4096,896]{1,0:T(8,128)(2,1)} %refs_1_.1) | copy-start | bytes 22020100
  103.6 100.8 %slice-start = ((s8[17432576]{0:T(1024)(128)(4,1)}), s8[4194304]{0:T(1024)(128)(4,1)S(1)}, s32[]{:S(2)}) async-start(s8[17432576]{0:T(1024)(128)(4,1)} %bitcast.37), calls=%async_computation | async-start | bytes 8388608
  103.6 100.8 %slice-start.1 = ((s8[17432576]{0:T(1024)(128)(4,1)}), s8[655360]{0:T(1024)(128)(4,1)S(1)}, s32[]{:S(2)}) async-start(s8[17432576]{0:T(1024)(128)(4,1)} %bitcast.37), calls=%async_computation.1 | async-start | bytes 1310720
  154.8 49.7 %slice-start.2 = ((s8[17432576]{0:T(1024)(128)(4,1)}), s8[4194304]{0:T(1024)(128)(4,1)S(1)}, s32[]{:S(2)}) async-start(s8[17432576]{0:T(1024)(128)(4,1)} %bitcast.37), calls=%async_computation.2 | async-start | bytes 8388608
  154.8 49.7 %slice-start.3 = ((s8[17432576]{0:T(1024)(128)(4,1)}), s8[4194304]{0:T(1024)(128)(4,1)S(1)}, s32[]{:S(2)}) async-start(s8[17432576]{0:T(1024)(128)(4,1)} %bitcast.37), calls=%async_computation.3 | async-start | bytes 8388608
  154.8 49.7 %slice-start.4 = ((s8[17432576]{0:T(1024)(128)(4,1)}), s8[4194304]{0:T(1024)(128)(4,1)S(1)}, s32[]{:S(2)}) async-start(s8[17432576]{0:T(1024)(128)(4,1)} %bitcast.37), calls=%async_computation.4 | async-start | bytes 8388608
  884.2 16.8 %slice-start.5 = ((s8[17432576]{0:T(1024)(128)(4,1)}), s8[4194304]{0:T(1024)(128)(4,1)S(1)}, s32[]{:S(2)}) async-start(s8[17432576]{0:T(1024)(128)(4,1)} %bitcast.39), calls=%async_computation.5 | async-start | bytes 8388608
  884.2 16.8 %slice-start.6 = ((s8[17432576]{0:T(1024)(128)(4,1)}), s8[4194304]{0:T(1024)(128)(4,1)S(1)}, s32[]{:S(2)}) async-start(s8[17432576]{0:T(1024)(128)(4,1)} %bitcast.39), calls=%async_computation.6 | async-start | bytes 8388608
  884.2 16.8 %slice-start.7 = ((s8[17432576]{0:T(1024)(128)(4,1)}), s8[4194304]{0:T(1024)(128)(4,1)S(1)}, s32[]{:S(2)}) async-start(s8[17432576]{0:T(1024)(128)(4,1)} %bitcast.39), calls=%async_computation.7 | async-start | bytes 8388608
  884.2 16.8 %slice-start.8 = ((s8[17432576]{0:T(1024)(128)(4,1)}), s8[4194304]{0:T(1024)(128)(4,1)S(1)}, s32[]{:S(2)}) async-start(s8[17432576]{0:T(1024)(128)(4,1)} %bitcast.39), calls=%async_computation.8 | async-start | bytes 8388608
  884.2 16.8 %slice-start.9 = ((s8[17432576]{0:T(1024)(128)(4,1)}), s8[655360]{0:T(1024)(128)(4,1)S(1)}, s32[]{:S(2)}) async-start(s8[17432576]{0:T(1024)(128)(4,1)} %bitcast.39), calls=%async_computation.9 | async-start | bytes 1310720
  901.0 7.3 copy-start.5
  901.0 8.7 copy-start.4
  908.3 2.7 copy-start.3
  908.4 4.2 copy-start.2
  908.4 5.6 copy-start.1
  909.7 5.7 copy-start

commit v2 on v1

--- a/solution.py
+++ b/solution.py
@@ -140,7 +140,7 @@
                 acc[rows, :] += dot_last(grad, wu_ref[...])
             return carry
 
-        lax.fori_loop(0, TOKENS // BLOCK, block, 0)
+        lax.fori_loop(0, TOKENS // BLOCK, block, 0, unroll=TOKENS // BLOCK)
         tile = jnp.dot(left_ref[...], qbuf[...], preferred_element_type=F32)
         slot = lax.rem(step, 2)
         for i in range(GROUP):
@@ -199,14 +199,14 @@
     ]
 
 
-def backward_block(pre_act, grad, w_down, left, grad_down, w_up, collective_id):
+def backward_block(pre_act, grad, w_down, left, grad_down, w_up, layer, collective_id):
     has_dx = w_up is not None
     last = STEPS - 1
     whole = pl.Buffered(buffer_count=1)
     in_specs = [
         pl.BlockSpec((TOKENS, TILE), lambda s: (0, jnp.minimum(s, last))),
         pl.BlockSpec((TOKENS, D), lambda s: (0, 0), pipeline_mode=whole),
-        pl.BlockSpec((TILE, D), lambda s: (jnp.minimum(s, last), 0)),
+        pl.BlockSpec((None, TILE, D), lambda s: (layer, jnp.minimum(s, last), 0)),
         pl.BlockSpec((D, TOKENS), lambda s: (0, 0), pipeline_mode=whole),
         pl.BlockSpec(memory_space=pl.ANY),
     ]
@@ -215,7 +215,7 @@
     out_specs = [pl.BlockSpec((UP_ROWS, FF), lambda s: (0, 0)), pl.BlockSpec((DOWN_ROWS, D), lambda s: (0, 0))]
     scratch = [pltpu.VMEM((TOKENS, TILE), BF16)]
     if has_dx:
-        in_specs.append(pl.BlockSpec((D, TILE), lambda s: (0, jnp.minimum(s, last))))
+        in_specs.append(pl.BlockSpec((None, D, TILE), lambda s: (layer, 0, jnp.minimum(s, last))))
         args.append(w_up)
         out_shape.append(jax.ShapeDtypeStruct((TOKENS, D), BF16))
         out_specs.append(pl.BlockSpec(memory_space=pl.ANY))
@@ -393,9 +393,9 @@
         z_three = jnp.dot(hidden, w_up[1], preferred_element_type=F32)
         act_three = gelu_parts(z_three)[0].astype(BF16)
         g_four = jnp.dot(act_three.T, grad_out, preferred_element_type=F32)
-        shard_three, shard_four, d_hidden = backward_block(z_three, grad_out, w_down[1], hidden.T, g_four, w_up[1], 1)
+        shard_three, shard_four, d_hidden = backward_block(z_three, grad_out, w_down, hidden.T, g_four, w_up, 1, 1)
         g_two = jnp.dot(act_one.T, d_hidden, preferred_element_type=F32)
-        shard_one, shard_two = backward_block(z_one, d_hidden, w_down[0], act_in.T, g_two, None, 2)
+        shard_one, shard_two = backward_block(z_one, d_hidden, w_down, act_in.T, g_two, None, 0, 2)
         scalars = jnp.stack([learn_rate, clip_norm])
         outs = tail(scalars, (shard_one, shard_two, shard_three, shard_four), (master_up, master_down, exp_avg_up, exp_avg_down, exp_sq_up, exp_sq_down))
         new_w_up = outs[0].reshape(2, D, FF)

time: 925 us -> 798 us (0.86)
  Pallas kernels: 590 us -> 475 us
  local copies, waits for them, and re-layouts: 58.5 us -> 46.4 us
    pallas_call x2, Pallas kernels: 442 us -> 327 us  [backward_block(): pl.pallas_call(functools.partial(backward_kernel, has_dx), grid=(STEPS +...]
    squeeze x2 -> x0, local copies, waits for them, and re-layouts: 14 us -> none  [the longest x1 7.51 us: device_step(): z_three = jnp.dot(hidden, w_up[1], preferred_element_type=F32)]
    unnamed x43 -> x25, local copies, waits for them, and re-layouts: 43.3 us -> 45.2 us
where the time goes in v2:
time: 798 us; the launch traced here: 790 us
  Pallas kernels  475 us (60%)
  matrix products  266 us (33%)
  local copies, waits for them, and re-layouts  46.4 us (6%)
    pallas_call x2, Pallas kernels, backward_block(): pl.pallas_call(functools.partial(backward_kernel, has_dx), grid=(STEPS +...  327 us
    pallas_call x1, Pallas kernels, tail(): pl.pallas_call(tail_kernel, in_specs=[pl.BlockSpec(memory_space=pltpu.SME...  148 us
    dot_general x1, matrix products, device_step(): g_two = jnp.dot(act_one.T, d_hidden, preferred_element_type=F32)  62 us
    dot_general x1, matrix products, device_step(): z_one = jnp.dot(act_in, w_up[0], preferred_element_type=F32)  59.3 us
    dot_general x1, matrix products, device_step(): z_three = jnp.dot(hidden, w_up[1], preferred_element_type=F32)  51.1 us
    dot_general x1, matrix products, device_step(): g_four = jnp.dot(act_three.T, grad_out, preferred_element_type=F32)  49.5 us
    unnamed x25, local copies, waits for them, and re-layouts  45.2 us
    dot_general x1, matrix products, device_step(): jnp.dot(act_one, w_down[0], preferred_element_type=F32).astype(BF16)  43.6 us

profile of v2, /device:TPU:0, one launch (start us, length us, event | category | flops | bytes accessed | tf_op | source)
XLA Modules:
  0.0 789.7 jit_solution(12134442631459512157)
XLA Ops:
  0.6 59.3 %multiply_convert_fusion.1 = (bf16[4096,4864]{1,0:T(8,128)(2,1)}, f32[4096,4864]{1,0:T(8,128)}) fusion(bf16[4096,896]{1,0:T(8,128)(2,1)} %param.12, bf16[2,896,4864]{2,1,0:T(8,128)(2,1)} %refs_5_.1), kind=kOutput, calls=%fused_computation.1 | convolution fusion | flops 35801530368 | bytes 135593984 | tf_op jit(solution)/shard_map/dot_general | solution.py:390
  60.0 43.6 %fusion.10 = bf16[4096,896]{0,1:T(8,128)(2,1)} fusion(bf16[4096,4864]{1,0:T(8,128)(2,1)} %get-tuple-element.37, bf16[2,4864,896]{2,1,0:T(8,128)(2,1)} %refs_2_.3), kind=kOutput, calls=%fused_computation.12 | convolution fusion | flops 35705585664 | bytes 55902208 | tf_op jit(solution)/shard_map/dot_general | solution.py:392
  103.5 0.0 copy-start.7
  103.5 51.1 %fusion.1.refs_0_ = f32[4096,4864]{1,0:T(8,128)} fusion(bf16[4096,896]{0,1:T(8,128)(2,1)} %fusion.10, bf16[2,896,4864]{2,1,0:T(8,128)(2,1)} %refs_5_.1), kind=kOutput, calls=%fused_computation.3 | convolution fusion | flops 35701915648 | bytes 95748096 | tf_op jit(solution)/shard_map/dot_general | solution.py:393
  154.6 0.0 copy-done.7
  154.6 49.5 %fusion = f32[4864,896]{1,0:T(8,128)} fusion(bf16[4096,896]{1,0:T(8,128)(2,1)S(1)} %copy-done.7, f32[4096,4864]{1,0:T(8,128)} %fusion.1.refs_0_), kind=kOutput, calls=%fused_computation.2 | convolution fusion | flops 35801530368 | bytes 104464384 | tf_op jit(solution)/shard_map/dot_general | solution.py:395
  204.1 185.5 %shard_map.187 = (f32[56,4864]{1,0:T(8,128)}, f32[304,896]{1,0:T(8,128)}, bf16[4096,896]{1,0:T(8,128)(2,1)}) custom-call(f32[4096,4864]{1,0:T(8,128)} %fusion.1.refs_0_, bf16[4096,896]{1,0:T(8,128)(2,1)} %refs_1_.1, bf16[2,4864,896]{2,1,0:T(8,128)(2,1)} %refs_2_.3, bf16[896,4096]{1,0:T(8,128)(2,1)} %bitcast.42, f32[8,2,304,896]{3,2,1,0:T(8,128)} %bitcast.41, ...), custom_call_target="tpu_custom_call" | custom-call | flops 107105746944 | bytes 157286400 | tf_op jit(solution)/shard_map/pallas_call | solution.py:225
  389.6 62.0 %fusion.16 = f32[4864,896]{1,0:T(8,128)} fusion(bf16[4096,4864]{1,0:T(8,128)(2,1)} %get-tuple-element.37, bf16[4096,896]{1,0:T(8,128)(2,1)} %get-tuple-element.23.refs_1_), kind=kOutput, calls=%fused_computation.17 | convolution fusion | flops 35701915648 | bytes 64618496 | tf_op jit(solution)/shard_map/dot_general | solution.py:397
  451.6 10.8 %copy.22 = bf16[4096,896]{0,1:T(8,128)(2,1)} copy(bf16[4096,896]{1,0:T(8,128)(2,1)} %param.12) | data formatting | bytes 14680064 | tf_op args[0]
  462.4 141.1 %shard_map.188 = (f32[56,4864]{1,0:T(8,128)}, f32[304,896]{1,0:T(8,128)}) custom-call(f32[4096,4864]{1,0:T(8,128)} %get-tuple-element.38.refs_0_, bf16[4096,896]{1,0:T(8,128)(2,1)} %get-tuple-element.23.refs_1_, bf16[2,4864,896]{2,1,0:T(8,128)(2,1)} %refs_2_.3, bf16[896,4096]{1,0:T(8,128)(2,1)} %bitcast.39, f32[8,2,304,896]{3,2,1,0:T(8,128)} %bitcast.40), custom_call_target="tpu_custom_call" | custom-call | flops 71403831296 | bytes 157286400 | tf_op jit(solution)/shard_map/pallas_call | solution.py:225
  604.9 0.6 pad_maximum_fusion.scalars
  605.4 148.2 %shard_map.189 = (bf16[2,2,2,2,2,56,4864]{6,5,4,3,2,1,0:T(8,128)(2,1)}, bf16[2,2,2,2,2,304,896]{6,5,4,3,2,1,0:T(8,128)(2,1)}, f32[2,56,4864]{2,1,0:T(8,128)}, f3...) custom-call(f32[2]{0:T(128)} %pad_maximum_fusion.scalars, ...), custom_call_target="tpu_custom_call" | custom-call | tf_op jit(solution)/shard_map/pallas_call | solution.py:364
  753.7 1.2 slice.15
  754.9 0.0 copy-start
  754.9 15.0 %copy.34 = bf16[2,896,4864]{2,1,0:T(8,128)(2,1)} copy(bf16[2,896,4864]{2,1,0:T(8,128)(2,1)} %bitcast.38) | data formatting | bytes 34865152
  769.9 2.5 copy-done
  772.4 0.0 copy-start.6
  772.4 0.0 copy-start.5
  772.4 0.0 copy-start.4
  772.4 0.0 copy-start.3
  772.4 8.8 %copy.35 = bf16[2,4864,896]{2,1,0:T(8,128)(2,1)} copy(bf16[2,4864,896]{2,1,0:T(8,128)(2,1)S(1)} %bitcast.37) | data formatting | bytes 34865152
  781.2 0.0 copy-done.6
  781.2 0.0 copy-start.2
  781.2 0.0 copy-start.1
  781.2 1.3 copy.36
  782.6 0.0 copy-done.5
  782.6 1.3 copy.37
  783.9 0.0 copy-done.4
  783.9 1.3 copy.38
  785.3 0.0 copy-done.3
  785.3 1.3 copy.39
  786.6 0.0 copy-done.2
  786.6 1.3 copy.40
  788.0 0.0 copy-done.1
  788.0 1.3 copy.41
Async XLA Ops:
  103.5 51.1 %copy-start.7 = (bf16[4096,896]{1,0:T(8,128)(2,1)S(1)}, bf16[4096,896]{1,0:T(8,128)(2,1)}, u32[]{:S(2)}) copy-start(bf16[4096,896]{1,0:T(8,128)(2,1)} %refs_1_.1) | copy-start | bytes 22020100
  754.9 17.5 %copy-start = (bf16[2,2,2,2,2,304,896]{6,5,4,3,2,1,0:T(8,128)(2,1)S(1)}, bf16[2,2,2,2,2,304,896]{6,5,4,3,2,1,0:T(8,128)(2,1)}, u32[]{:S(2)}) copy-start(bf16[2,2,2,2,2,304,896]{6,5,4,3,2,1,0:T(8,128)(2,1)} %get-tuple-element.29) | copy-start | bytes 52297732
  772.4 8.8 %copy-start.6 = (f32[2,56,4864]{2,1,0:T(8,128)S(1)}, f32[2,56,4864]{2,1,0:T(8,128)}, u32[]{:S(2)}) copy-start(f32[2,56,4864]{2,1,0:T(8,128)} %get-tuple-element.50) | copy-start | bytes 6537220
  772.4 10.2 %copy-start.5 = (f32[2,304,896]{2,1,0:T(8,128)S(1)}, f32[2,304,896]{2,1,0:T(8,128)}, u32[]{:S(2)}) copy-start(f32[2,304,896]{2,1,0:T(8,128)} %get-tuple-element.51) | copy-start | bytes 6537220
  772.4 11.5 %copy-start.4 = (f32[2,56,4864]{2,1,0:T(8,128)S(1)}, f32[2,56,4864]{2,1,0:T(8,128)}, u32[]{:S(2)}) copy-start(f32[2,56,4864]{2,1,0:T(8,128)} %get-tuple-element.52) | copy-start | bytes 6537220
  772.4 12.9 %copy-start.3 = (f32[2,304,896]{2,1,0:T(8,128)S(1)}, f32[2,304,896]{2,1,0:T(8,128)}, u32[]{:S(2)}) copy-start(f32[2,304,896]{2,1,0:T(8,128)} %get-tuple-element.53) | copy-start | bytes 6537220
  781.2 5.4 copy-start.2
  781.2 6.7 copy-start.1

commit v3 on v2

--- a/solution.py
+++ b/solution.py
@@ -99,19 +99,52 @@
             return self.sums[held, 0] + self.landed[2][lax.rem(unit, SLOTS), 0]
 
 
-def within(unit):
-    return jnp.logical_and(unit >= 0, unit < STEPS)
-
-
-def backward_kernel(has_dx, *refs):
-    if has_dx:
-        z_ref, dy_ref, wd_ref, left_ref, gd_ref, wu_ref, up_ref, down_ref, dx_ref = refs[:9]
-        qbuf, acc, stage_buf = refs[9:12]
-        rest = refs[12:]
-    else:
-        z_ref, dy_ref, wd_ref, left_ref, gd_ref, up_ref, down_ref = refs[:7]
-        qbuf = refs[7]
-        rest = refs[8:]
+def within(unit, count):
+    return jnp.logical_and(unit >= 0, unit < count)
+
+
+def advance(ring, tick, count, emit):
+    @pl.when(within(tick - DRAIN, count))
+    def _():
+        emit(tick - DRAIN, ring.finish(3, tick - DRAIN))
+
+    for stage in (2, 1, 0):
+        unit = tick - 1 - stage * LAG
+
+        @pl.when(within(unit, count))
+        def _():
+            ring.finish(stage, unit)
+            ring.copy(stage + 1, unit).start()
+
+
+def greet_partners(ring):
+    me, core, chip = ring.me, ring.core, ring.chip
+    greet([me + 1 - 2 * core] + [me + 2 * s * (1 - 2 * lax.rem(chip // s, 2)) for s in (1, 2, 4)])
+
+
+def aligned(index, size):
+    return pl.ds(pl.multiple_of(index * size, size), size)
+
+
+def grad_tile(z_ref, dy_ref, wd_ref, qbuf, extra):
+    def block(index, carry):
+        rows = aligned(index, BLOCK)
+        slope = gelu_parts(z_ref[rows, :])[1]
+        grad = (dot_last(dy_ref[rows, :], wd_ref[...]) * slope).astype(BF16)
+        qbuf[rows, :] = grad
+        extra(rows, grad)
+        return carry
+
+    lax.fori_loop(0, TOKENS // BLOCK, block, 0, unroll=TOKENS // BLOCK)
+
+
+def store_tile(left, qbuf, gbuf, slot):
+    tile = jnp.dot(left[...], qbuf[...], preferred_element_type=F32)
+    for i in range(GROUP):
+        gbuf[slot, i // 2, i % 2] = tile[i * UP_ROWS:(i + 1) * UP_ROWS, :]
+
+
+def second_block_kernel(z_ref, dy_ref, wd_ref, left_ref, gd_ref, wu_ref, up_ref, down_ref, dx_ref, dxt_ref, qbuf, acc, stage_buf, stage_t, *rest):
     up = ReduceScatter(0, *rest[0:8])
     down = ReduceScatter(1, *rest[8:16])
     load_sem, out_sem = rest[16:18]
@@ -119,47 +152,30 @@
 
     def load(unit):
         slot = lax.rem(unit, 2)
-        return pltpu.make_async_copy(gd_ref.at[:, :, pl.ds(pl.multiple_of(unit * DOWN_UNIT, DOWN_UNIT), DOWN_UNIT)], down.gbuf.at[slot], load_sem.at[slot])
+        return pltpu.make_async_copy(gd_ref.at[:, :, aligned(unit, DOWN_UNIT)], down.gbuf.at[slot], load_sem.at[slot])
 
     @pl.when(step == 0)
     def _():
-        me, core, chip = up.me, up.core, up.chip
-        greet([me + 1 - 2 * core] + [me + 2 * s * (1 - 2 * lax.rem(chip // s, 2)) for s in (1, 2, 4)])
+        greet_partners(up)
         load(0).start()
-        if has_dx:
-            acc[...] = jnp.zeros_like(acc)
+        acc[...] = jnp.zeros_like(acc)
+
+    def add_dx(rows, grad):
+        acc[rows, :] += dot_last(grad, wu_ref[...])
 
     @pl.when(step < STEPS)
     def _():
-        def block(index, carry):
-            rows = pl.ds(pl.multiple_of(index * BLOCK, BLOCK), BLOCK)
-            slope = gelu_parts(z_ref[rows, :])[1]
-            grad = (dot_last(dy_ref[rows, :], wd_ref[...]) * slope).astype(BF16)
-            qbuf[rows, :] = grad
-            if has_dx:
-                acc[rows, :] += dot_last(grad, wu_ref[...])
-            return carry
-
-        lax.fori_loop(0, TOKENS // BLOCK, block, 0, unroll=TOKENS // BLOCK)
-        tile = jnp.dot(left_ref[...], qbuf[...], preferred_element_type=F32)
-        slot = lax.rem(step, 2)
-        for i in range(GROUP):
-            up.gbuf[slot, i // 2, i % 2] = tile[i * UP_ROWS:(i + 1) * UP_ROWS, :]
-
-    @pl.when(within(step - DRAIN))
-    def _():
-        unit = step - DRAIN
-        up_ref[:, pl.ds(pl.multiple_of(unit * TILE, TILE), TILE)] = up.finish(3, unit)
-        down_ref[pl.ds(pl.multiple_of(unit * DOWN_UNIT, DOWN_UNIT), DOWN_UNIT), :] = down.finish(3, unit)
-
-    for stage in (2, 1, 0):
-        unit = step - 1 - stage * LAG
-
-        @pl.when(within(unit))
-        def _():
-            for ring in (up, down):
-                ring.finish(stage, unit)
-                ring.copy(stage + 1, unit).start()
+        grad_tile(z_ref, dy_ref, wd_ref, qbuf, add_dx)
+        store_tile(left_ref, qbuf, up.gbuf, lax.rem(step, 2))
+
+    def emit_up(unit, block):
+        up_ref[:, aligned(unit, TILE)] = block
+
+    def emit_down(unit, block):
+        down_ref[aligned(unit, DOWN_UNIT), :] = block
+
+    advance(up, step, STEPS, emit_up)
+    advance(down, step, STEPS, emit_down)
 
     @pl.when(step < STEPS - 1)
     def _():
@@ -171,18 +187,110 @@
         load(step).wait()
         down.copy(0, step).start()
 
-    if has_dx:
-        @pl.when(step == STEPS - 1)
+    @pl.when(step == STEPS - 1)
+    def _():
+        def flush(index, carry):
+            rows = aligned(index, BLOCK)
+            value = acc[rows, :]
+            stage_buf[...] = value.astype(BF16)
+            stage_t[...] = value.T.astype(BF16)
+            outs = [pltpu.make_async_copy(stage_buf, dx_ref.at[rows, :], out_sem.at[0]), pltpu.make_async_copy(stage_t, dxt_ref.at[:, rows], out_sem.at[1])]
+            for out in outs:
+                out.start()
+            for out in outs:
+                out.wait()
+            return carry
+
+        lax.fori_loop(0, TOKENS // BLOCK, flush, 0)
+
+
+def first_block_kernel(z_ref, dy_ref, wd_ref, dyt_ref, act_ref, x_ref, up_ref, down_ref, gd_ref, qbuf, left, stage_buf, *rest):
+    up = ReduceScatter(0, *rest[0:8])
+    down = ReduceScatter(1, *rest[8:16])
+    load_sem, out_sem = rest[16:18]
+    step = pl.program_id(0)
+
+    def loads(unit):
+        slot = lax.rem(unit, 2)
+        columns, half = aligned(unit // 2, LANES), lax.rem(unit, 2) * HALF_ROWS
+        copies = []
+        for i in range(GROUP):
+            rows = pl.ds(pl.multiple_of(i * DOWN_ROWS + half, 8), HALF_ROWS)
+            copies.append(pltpu.make_async_copy(gd_ref.at[rows, columns], down.gbuf.at[slot, i // 2, i % 2], load_sem.at[slot, i]))
+        return copies
+
+    def write(index, split):
+        slot = lax.rem(index, 2)
+        rows = aligned(lax.rem(index, STEPS), TILE)
+        if split == 0:
+            return pltpu.make_async_copy(stage_buf.at[slot, :, pl.ds(0, SPLIT)], gd_ref.at[rows, pl.ds(0, SPLIT)], out_sem.at[slot])
+        return pltpu.make_async_copy(stage_buf.at[slot, :, pl.ds(0, D - SPLIT)], gd_ref.at[rows, pl.ds(SPLIT, D - SPLIT)], out_sem.at[slot])
+
+    @pl.when(step == 0)
+    def _():
+        greet_partners(up)
+
+    @pl.when(step < TOKENS // TILE)
+    def _():
+        left[:, aligned(step, TILE)] = x_ref[...].T
+
+    for split in (0, 1):
+        @pl.when(within(step - split * STEPS, STEPS))
         def _():
-            def flush(index, carry):
-                rows = pl.ds(pl.multiple_of(index * BLOCK, BLOCK), BLOCK)
-                stage_buf[...] = acc[rows, :].astype(BF16)
-                out = pltpu.make_async_copy(stage_buf, dx_ref.at[rows, :], out_sem)
-                out.start()
-                out.wait()
-                return carry
-
-            lax.fori_loop(0, TOKENS // BLOCK, flush, 0)
+            width = SPLIT if split == 0 else D - SPLIT
+            part = jnp.dot(dyt_ref[pl.ds(split * SPLIT, width), :], act_ref[...], preferred_element_type=F32)
+            stage_buf[lax.rem(step, 2), :, pl.ds(0, width)] = part.T
+
+    for split in (0, 1):
+        @pl.when(within(step - 1 - split * STEPS, STEPS))
+        def _():
+            write(step - 1, split).wait()
+
+    for split in (0, 1):
+        @pl.when(within(step - split * STEPS, STEPS))
+        def _():
+            write(step, split).start()
+
+    tile = step - 2 * STEPS
+
+    @pl.when(within(tile, STEPS))
+    def _():
+        grad_tile(z_ref, dy_ref, wd_ref, qbuf, lambda rows, grad: None)
+        store_tile(left, qbuf, up.gbuf, lax.rem(tile, 2))
+
+    def emit_up(unit, block):
+        up_ref[:, aligned(unit, TILE)] = block
+
+    def emit_down(unit, block):
+        down_ref[pl.ds(pl.multiple_of(lax.rem(unit, 2) * HALF_ROWS, 8), HALF_ROWS), aligned(unit // 2, LANES)] = block
+
+    early = step - FIRST_TICK
+    ticking = jnp.logical_or(jnp.logical_and(early >= 0, lax.rem(early, TICK_GAP) == 0), tile >= 0)
+    tick = jnp.where(tile >= 0, tile + (2 * STEPS - FIRST_TICK) // TICK_GAP, early // TICK_GAP)
+    tick = jnp.where(ticking, tick, -1)
+
+    advance(up, tile, STEPS, emit_up)
+    advance(down, tick, DOWN_UNITS, emit_down)
+
+    @pl.when(step == FIRST_TICK - 1)
+    def _():
+        for copy in loads(0):
+            copy.start()
+
+    @pl.when(within(tick, DOWN_UNITS - 1))
+    def _():
+        for copy in loads(tick + 1):
+            copy.start()
+
+    @pl.when(within(tile, STEPS))
+    def _():
+        up.copy(0, tile).start()
+
+    @pl.when(within(tick, DOWN_UNITS))
+    def _():
+        for copy in loads(tick):
+            copy.wait()
+        down.copy(0, tick).start()
 
 
 def ring_scratch(rows, columns):
@@ -199,39 +307,62 @@
     ]
 
 
-def backward_block(pre_act, grad, w_down, left, grad_down, w_up, layer, collective_id):
-    has_dx = w_up is not None
+WHOLE = pl.Buffered(buffer_count=1)
+ANY = pl.BlockSpec(memory_space=pl.ANY)
+
+
+def params(collective_id):
+    return pltpu.CompilerParams(collective_id=collective_id, has_side_effects=True, vmem_limit_bytes=67043328, dimension_semantics=("arbitrary",))
+
+
+def second_block(pre_act, grad, w_down, left, grad_down, w_up):
     last = STEPS - 1
-    whole = pl.Buffered(buffer_count=1)
-    in_specs = [
-        pl.BlockSpec((TOKENS, TILE), lambda s: (0, jnp.minimum(s, last))),
-        pl.BlockSpec((TOKENS, D), lambda s: (0, 0), pipeline_mode=whole),
-        pl.BlockSpec((None, TILE, D), lambda s: (layer, jnp.minimum(s, last), 0)),
-        pl.BlockSpec((D, TOKENS), lambda s: (0, 0), pipeline_mode=whole),
-        pl.BlockSpec(memory_space=pl.ANY),
-    ]
-    args = [pre_act, grad, w_down, left, grad_down.reshape(8, 2, DOWN_ROWS, D)]
-    out_shape = [jax.ShapeDtypeStruct((UP_ROWS, FF), F32), jax.ShapeDtypeStruct((DOWN_ROWS, D), F32)]
-    out_specs = [pl.BlockSpec((UP_ROWS, FF), lambda s: (0, 0)), pl.BlockSpec((DOWN_ROWS, D), lambda s: (0, 0))]
-    scratch = [pltpu.VMEM((TOKENS, TILE), BF16)]
-    if has_dx:
-        in_specs.append(pl.BlockSpec((None, D, TILE), lambda s: (layer, 0, jnp.minimum(s, last))))
-        args.append(w_up)
-        out_shape.append(jax.ShapeDtypeStruct((TOKENS, D), BF16))
-        out_specs.append(pl.BlockSpec(memory_space=pl.ANY))
-        scratch += [pltpu.VMEM((TOKENS, D), F32), pltpu.VMEM((BLOCK, D), BF16)]
-    scratch += ring_scratch(UP_ROWS, TILE) + ring_scratch(DOWN_UNIT, D)
-    scratch += [pltpu.SemaphoreType.DMA((2,)), pltpu.SemaphoreType.DMA]
     return pl.pallas_call(
-        functools.partial(backward_kernel, has_dx),
+        second_block_kernel,
         grid=(STEPS + DRAIN,),
-        in_specs=in_specs,
-        out_specs=out_specs,
-        out_shape=out_shape,
-        scratch_shapes=scratch,
-        compiler_params=pltpu.CompilerParams(collective_id=collective_id, has_side_effects=True, vmem_limit_bytes=67043328, dimension_semantics=("arbitrary",)),
-        cost_estimate=pl.CostEstimate(flops=(6 if has_dx else 4) * TOKENS * D * FF, bytes_accessed=150 * 2**20, transcendentals=2 * TOKENS * FF),
-    )(*args)
+        in_specs=[
+            pl.BlockSpec((TOKENS, TILE), lambda s: (0, jnp.minimum(s, last))),
+            pl.BlockSpec((TOKENS, D), lambda s: (0, 0), pipeline_mode=WHOLE),
+            pl.BlockSpec((None, TILE, D), lambda s: (1, jnp.minimum(s, last), 0)),
+            pl.BlockSpec((D, TOKENS), lambda s: (0, 0), pipeline_mode=WHOLE),
+            ANY,
+            pl.BlockSpec((None, D, TILE), lambda s: (1, 0, jnp.minimum(s, last))),
+        ],
+        out_specs=[pl.BlockSpec((UP_ROWS, FF), lambda s: (0, 0)), pl.BlockSpec((DOWN_ROWS, D), lambda s: (0, 0)), ANY, ANY],
+        out_shape=[jax.ShapeDtypeStruct((UP_ROWS, FF), F32), jax.ShapeDtypeStruct((DOWN_ROWS, D), F32), jax.ShapeDtypeStruct((TOKENS, D), BF16), jax.ShapeDtypeStruct((D, TOKENS), BF16)],
+        scratch_shapes=[pltpu.VMEM((TOKENS, TILE), BF16), pltpu.VMEM((TOKENS, D), F32), pltpu.VMEM((BLOCK, D), BF16), pltpu.VMEM((D, BLOCK), BF16)] + ring_scratch(UP_ROWS, TILE) + ring_scratch(DOWN_UNIT, D) + [pltpu.SemaphoreType.DMA((2,)), pltpu.SemaphoreType.DMA((2,))],
+        compiler_params=params(1),
+        cost_estimate=pl.CostEstimate(flops=6 * TOKENS * D * FF, bytes_accessed=150 * 2**20, transcendentals=2 * TOKENS * FF),
+    )(pre_act, grad, w_down, left, grad_down.reshape(8, 2, DOWN_ROWS, D), w_up)
+
+
+LANES = 128
+HALF_ROWS = DOWN_ROWS // 2
+DOWN_UNITS = 2 * D // LANES
+SPLIT = 512
+TICK_GAP = 4
+FIRST_TICK = STEPS + 3
+
+
+def first_block(pre_act, grad, w_down, grad_t, act, act_in):
+    start, last = 2 * STEPS, STEPS - 1
+    return pl.pallas_call(
+        first_block_kernel,
+        grid=(start + STEPS + DRAIN,),
+        in_specs=[
+            pl.BlockSpec((TOKENS, TILE), lambda s: (0, jnp.clip(s - start, 0, last))),
+            pl.BlockSpec((TOKENS, D), lambda s: (0, 0), pipeline_mode=WHOLE),
+            pl.BlockSpec((None, TILE, D), lambda s: (0, jnp.clip(s - start, 0, last), 0)),
+            pl.BlockSpec((D, TOKENS), lambda s: (0, 0), pipeline_mode=WHOLE),
+            pl.BlockSpec((TOKENS, TILE), lambda s: (0, lax.rem(jnp.minimum(s, start - 1), STEPS))),
+            pl.BlockSpec((TILE, D), lambda s: (jnp.minimum(s, TOKENS // TILE - 1), 0)),
+        ],
+        out_specs=[pl.BlockSpec((UP_ROWS, FF), lambda s: (0, 0)), pl.BlockSpec((DOWN_ROWS, D), lambda s: (0, 0)), ANY],
+        out_shape=[jax.ShapeDtypeStruct((UP_ROWS, FF), F32), jax.ShapeDtypeStruct((DOWN_ROWS, D), F32), jax.ShapeDtypeStruct((FF, D), F32)],
+        scratch_shapes=[pltpu.VMEM((TOKENS, TILE), BF16), pltpu.VMEM((D, TOKENS), BF16), pltpu.VMEM((2, TILE, SPLIT), F32)] + ring_scratch(UP_ROWS, TILE) + ring_scratch(HALF_ROWS, LANES) + [pltpu.SemaphoreType.DMA((2, GROUP)), pltpu.SemaphoreType.DMA((2,))],
+        compiler_params=params(2),
+        cost_estimate=pl.CostEstimate(flops=6 * TOKENS * D * FF, bytes_accessed=250 * 2**20, transcendentals=2 * TOKENS * FF),
+    )(pre_act, grad, w_down, grad_t, act, act_in)
 
 
 COLUMN_PARTS = ((0, 1664), (1664, 1664), (3328, 1536))
@@ -240,7 +371,15 @@
 CHUNKS = 12
 
 
-def tail_kernel(scalars, g1, g2, g3, g4, master_up, master_down, avg_up, avg_down, sq_up, sq_down, w_up_out, w_down_out, master_up_out, master_down_out, avg_up_out, avg_down_out, sq_up_out, sq_down_out, norm_out, send_up, send_down, dir_up, dir_down, mine, stats, stat_send, stat_recv, send_sem, recv_sem, own_sem):
+def tail_kernel(scalars, g1, g2, g3, g4, *refs):
+    states, (w_up_out, w_down_out), state_outs, norm_out = refs[:6], refs[6:8], refs[8:14], refs[14]
+    send_up, send_down, dir_up, dir_down, mine, stats, stat_send, stat_recv, send_sem, recv_sem, own_sem = refs[15:26]
+    held, (in_sem, out_sem) = refs[26:32], refs[32:34]
+    master_up, master_down, avg_up, avg_down, sq_up, sq_down = held
+    fetches = [pltpu.make_async_copy(src, dst, in_sem.at[i]) for i, (src, dst) in enumerate(zip(states, held))]
+    stores = [pltpu.make_async_copy(src, dst, out_sem.at[i]) for i, (src, dst) in enumerate(zip(held, state_outs))]
+    for copy in fetches:
+        copy.start()
     me = lax.axis_index("data")
     core = lax.rem(me, 2)
     coords = (me // 8, lax.rem(me // 4, 2), lax.rem(me // 2, 2))
@@ -275,17 +414,21 @@
     bias_two = 1.0 - BETA_TWO ** STEP
     lane = lax.broadcasted_iota(jnp.int32, (8, 128), 1)
     row = jnp.zeros((8, 128), F32)
-    families = ((master_up, avg_up, sq_up, avg_up_out, sq_up_out, dir_up), (master_down, avg_down, sq_down, avg_down_out, sq_down_out, dir_down))
-    for f, (master, avg, sq, avg_out, sq_out, direction) in enumerate(families):
+    families = ((master_up, avg_up, sq_up, dir_up), (master_down, avg_down, sq_down, dir_down))
+    for f, (master, avg, sq, direction) in enumerate(families):
+        for i in (f, 2 + f, 4 + f):
+            fetches[i].wait()
         for k in range(2):
             g = grads[f][k][...] * scale
             avg_new = BETA_ONE * avg[k] + (1.0 - BETA_ONE) * clip * g
             sq_new = BETA_TWO * sq[k] + (1.0 - BETA_TWO) * (clip * clip) * (g * g)
             u = (avg_new / bias_one) / (jnp.sqrt(sq_new / bias_two) + ADAM_EPS)
-            avg_out[k] = avg_new
-            sq_out[k] = sq_new
+            avg[k] = avg_new
+            sq[k] = sq_new
             direction[k] = u
             row = row + jnp.where(lane == 2 * f + k, sum_square(master[k]), 0.0) + jnp.where(lane == 4 + 2 * f + k, sum_square(u), 0.0)
+        stores[2 + f].start()
+        stores[4 + f].start()
     totals = share(1, row)
 
     def out_view(chunk, picks, flipped=None):
@@ -317,12 +460,12 @@
     pending = []
     rounds = [[], [], []]
     locals_ = []
-    for f, (master, master_out, direction, send) in enumerate(((master_up, master_up_out, dir_up, send_up), (master_down, master_down_out, dir_down, send_down))):
+    for f, (master, direction, send) in enumerate(((master_up, dir_up, send_up), (master_down, dir_down, send_down))):
         for k in range(2):
             i = 2 * f + k
             ratio = jnp.sqrt(totals[0:1, i:i + 1]) / jnp.sqrt(totals[0:1, 4 + i:5 + i])
             new = master[k] - scalars[0] * ratio * direction[k]
-            master_out[k] = new
+            master[k] = new
             send[k] = new.astype(BF16)
             for part in range(3):
                 n = 3 * i + part
@@ -338,6 +481,7 @@
                 pending[-1].start()
                 locals_.append(pltpu.make_async_copy(src, dst, own_sem.at[n]))
                 locals_[-1].start()
+        stores[f].start()
     for turn in range(3):
         for n in range(CHUNKS):
             first, second, third = order[n]
@@ -352,7 +496,7 @@
                 view = out_view(chunks[n], order[n][:turn + 1])
                 rounds[turn + 1].append(remote(n, turn + 1, view, view, neighbour(order[n][turn + 1])))
                 rounds[turn + 1][-1].start()
-    for copy in pending:
+    for copy in pending + stores:
         copy.wait()
 
 
@@ -363,8 +507,8 @@
     shape = jax.ShapeDtypeStruct
     return pl.pallas_call(
         tail_kernel,
-        in_specs=[pl.BlockSpec(memory_space=pltpu.SMEM)] + [vmem] * 10,
-        out_specs=[any_space] * 2 + [vmem] * 7,
+        in_specs=[pl.BlockSpec(memory_space=pltpu.SMEM)] + [vmem] * 4 + [any_space] * 6,
+        out_specs=[any_space] * 8 + [vmem],
         out_shape=[
             shape((2, 2, 2, 2, 2, UP_ROWS, FF), BF16),
             shape((2, 2, 2, 2, 2, DOWN_ROWS, D), BF16),
@@ -376,6 +520,7 @@
             pltpu.VMEM((2, 8, 128), F32), pltpu.VMEM((2, GROUP, 8, 128), F32),
             pltpu.SemaphoreType.DMA((2, GROUP)), pltpu.SemaphoreType.DMA((2, GROUP)),
             pltpu.SemaphoreType.DMA((CHUNKS, 7)), pltpu.SemaphoreType.DMA((CHUNKS, 7)), pltpu.SemaphoreType.DMA((CHUNKS,)),
+            *[pltpu.VMEM(dims, F32) for dims in (up, down) * 3], pltpu.SemaphoreType.DMA((6,)), pltpu.SemaphoreType.DMA((6,)),
         ],
         compiler_params=pltpu.CompilerParams(collective_id=3, has_side_effects=True, vmem_limit_bytes=67043328),
     )(scalars, *grads, *states)
@@ -393,9 +538,8 @@
         z_three = jnp.dot(hidden, w_up[1], preferred_element_type=F32)
         act_three = gelu_parts(z_three)[0].astype(BF16)
         g_four = jnp.dot(act_three.T, grad_out, preferred_element_type=F32)
-        shard_three, shard_four, d_hidden = backward_block(z_three, grad_out, w_down, hidden.T, g_four, w_up, 1, 1)
-        g_two = jnp.dot(act_one.T, d_hidden, preferred_element_type=F32)
-        shard_one, shard_two = backward_block(z_one, d_hidden, w_down, act_in.T, g_two, None, 0, 2)
+        shard_three, shard_four, d_hidden, d_hidden_t = second_block(z_three, grad_out, w_down, hidden.T, g_four, w_up)
+        shard_one, shard_two = first_block(z_one, d_hidden, w_down, d_hidden_t, act_one, act_in)[:2]
         scalars = jnp.stack([learn_rate, clip_norm])
         outs = tail(scalars, (shard_one, shard_two, shard_three, shard_four), (master_up, master_down, exp_avg_up, exp_avg_down, exp_sq_up, exp_sq_down))
         new_w_up = outs[0].reshape(2, D, FF)

time: 798 us -> 785 us (0.984)
  matrix products: 266 us -> 203 us
  Pallas kernels: 475 us -> 534 us
  local copies, waits for them, and re-layouts: 46.4 us -> 35.6 us
    pallas_call x2, Pallas kernels: 327 us -> 395 us  [the longest x1 204 us: first_block(): pl.pallas_call(first_block_kernel, grid=(start + STEPS + DRAIN,), in_spec...]
    dot_general x1 -> x0, matrix products: 62 us -> none  [device_step(): g_two = jnp.dot(act_one.T, d_hidden, preferred_element_type=F32)]
    unnamed x25 -> x24, local copies, waits for them, and re-layouts: 45.2 us -> 34.4 us
    pallas_call x1, Pallas kernels: 148 us -> 139 us  [tail(): pl.pallas_call(tail_kernel, in_specs=[pl.BlockSpec(memory_space=pltpu.SME...]
where the time goes in v3:
time: 785 us; the launch traced here: 776 us
  Pallas kernels  534 us (68%)
  matrix products  203 us (26%)
  local copies, waits for them, and re-layouts  35.6 us (5%)
    pallas_call x1, Pallas kernels, first_block(): pl.pallas_call(first_block_kernel, grid=(start + STEPS + DRAIN,), in_spec...  204 us
    pallas_call x1, Pallas kernels, second_block(): pl.pallas_call(second_block_kernel, grid=(STEPS + DRAIN,), in_specs=[pl.B...  191 us
    pallas_call x1, Pallas kernels, tail(): pl.pallas_call(tail_kernel, in_specs=[pl.BlockSpec(memory_space=pltpu.SME...  139 us
    dot_general x1, matrix products, device_step(): z_one = jnp.dot(act_in, w_up[0], preferred_element_type=F32)  59.3 us
    dot_general x1, matrix products, device_step(): z_three = jnp.dot(hidden, w_up[1], preferred_element_type=F32)  51 us
    dot_general x1, matrix products, device_step(): g_four = jnp.dot(act_three.T, grad_out, preferred_element_type=F32)  49.5 us
    dot_general x1, matrix products, device_step(): jnp.dot(act_one, w_down[0], preferred_element_type=F32).astype(BF16)  43.6 us
    unnamed x24, local copies, waits for them, and re-layouts  34.4 us

profile of v3, /device:TPU:0, one launch (start us, length us, event | category | flops | bytes accessed | tf_op | source)
XLA Modules:
  0.0 776.3 jit_solution(11707913993374657922)
XLA Ops:
  0.6 59.3 %multiply_convert_fusion.1 = (bf16[4096,4864]{1,0:T(8,128)(2,1)}, f32[4096,4864]{1,0:T(8,128)}) fusion(bf16[4096,896]{1,0:T(8,128)(2,1)} %x_ref.1, bf16[2,896,4864]{2,1,0:T(8,128)(2,1)} %wu_ref.1), kind=kOutput, calls=%fused_computation.1 | convolution fusion | flops 35801530368 | bytes 135593984 | tf_op jit(solution)/shard_map/dot_general | solution.py:535
  60.0 43.6 %fusion.10 = bf16[4096,896]{0,1:T(8,128)(2,1)} fusion(bf16[4096,4864]{1,0:T(8,128)(2,1)} %get-tuple-element.39.act_ref, bf16[2,4864,896]{2,1,0:T(8,128)(2,1)} %wd_ref.3), kind=kOutput, calls=%fused_computation.12 | convolution fusion | flops 35705585664 | bytes 55902208 | tf_op jit(solution)/shard_map/dot_general | solution.py:537
  103.5 0.0 copy-start.7
  103.5 51.0 %fusion.1.z_ref = f32[4096,4864]{1,0:T(8,128)} fusion(bf16[4096,896]{0,1:T(8,128)(2,1)} %fusion.10, bf16[2,896,4864]{2,1,0:T(8,128)(2,1)} %wu_ref.1), kind=kOutput, calls=%fused_computation.3 | convolution fusion | flops 35701915648 | bytes 95748096 | tf_op jit(solution)/shard_map/dot_general | solution.py:538
  154.5 0.0 copy-done.7
  154.5 49.5 %fusion = f32[4864,896]{1,0:T(8,128)} fusion(bf16[4096,896]{1,0:T(8,128)(2,1)S(1)} %copy-done.7, f32[4096,4864]{1,0:T(8,128)} %fusion.1.z_ref), kind=kOutput, calls=%fused_computation.2 | convolution fusion | flops 35801530368 | bytes 104464384 | tf_op jit(solution)/shard_map/dot_general | solution.py:540
  204.0 191.0 %shard_map.187 = (f32[56,4864]{1,0:T(8,128)}, f32[304,896]{1,0:T(8,128)}, bf16[4096,896]{1,0:T(8,128)(2,1)}, bf16[896,4096]{1,0:T(8,128)(2,1)}) custom-call(f32[4096,4864]{1,0:T(8,128)} %fusion.1.z_ref, bf16[4096,896]{1,0:T(8,128)(2,1)} %dy_ref.1, bf16[2,4864,896]{2,1,0:T(8,128)(2,1)} %wd_ref.3, bf16[896,4096]{1,0:T(8,128)(2,1)} %bitcast.36, ...), custom_call_target="tpu_custom_call" | custom-call | flops 107105746944 | bytes 157286400 | tf_op jit(solution)/shard_map/pallas_call | solution.py:320
  395.0 203.8 %shard_map.188 = (f32[56,4864]{1,0:T(8,128)}, f32[304,896]{1,0:T(8,128)}, f32[4864,896]{1,0:T(8,128)}) custom-call(f32[4096,4864]{1,0:T(8,128)} %get-tuple-element.40.z_ref, bf16[4096,896]{1,0:T(8,128)(2,1)} %get-tuple-element.24.dy_ref, bf16[2,4864,896]{2,1,0:T(8,128)(2,1)} %wd_ref.3, bf16[896,4096]{1,0:T(8,128)(2,1)} %get-tuple-element.25.dyt_ref, ...), custom_call_target="tpu_custom_call" | custom-call | flops 107105746944 | bytes 262144000 | tf_op jit(solution)/shard_map/pallas_call | solution.py:349
  600.1 0.6 pad_maximum_fusion.scalars
  600.7 139.5 %shard_map.189 = (bf16[2,2,2,2,2,56,4864]{6,5,4,3,2,1,0:T(8,128)(2,1)}, bf16[2,2,2,2,2,304,896]{6,5,4,3,2,1,0:T(8,128)(2,1)}, f32[2,56,4864]{2,1,0:T(8,128)}, f3...) custom-call(f32[2]{0:T(128)} %pad_maximum_fusion.scalars, ...), custom_call_target="tpu_custom_call" | custom-call | tf_op jit(solution)/shard_map/pallas_call | solution.py:508
  740.2 1.2 slice.15
  741.4 0.0 copy-start
  741.4 15.0 %copy.33 = bf16[2,896,4864]{2,1,0:T(8,128)(2,1)} copy(bf16[2,896,4864]{2,1,0:T(8,128)(2,1)} %bitcast.34) | data formatting | bytes 34865152
  756.3 2.5 copy-done
  758.9 0.0 copy-start.6
  758.9 0.0 copy-start.5
  758.9 0.0 copy-start.4
  758.9 0.0 copy-start.3
  758.9 8.8 %copy.34 = bf16[2,4864,896]{2,1,0:T(8,128)(2,1)} copy(bf16[2,4864,896]{2,1,0:T(8,128)(2,1)S(1)} %bitcast.33) | data formatting | bytes 34865152
  767.7 0.0 copy-done.6
  767.7 0.0 copy-start.2
  767.7 0.0 copy-start.1
  767.7 1.3 copy.35
  769.0 0.0 copy-done.5
  769.0 1.3 copy.36
  770.4 0.0 copy-done.4
  770.4 1.3 copy.37
  771.7 0.0 copy-done.3
  771.7 1.3 copy.38
  773.1 0.0 copy-done.2
  773.1 1.3 copy.39
  774.4 0.0 copy-done.1
  774.4 1.3 copy.40
Async XLA Ops:
  103.5 51.0 %copy-start.7 = (bf16[4096,896]{1,0:T(8,128)(2,1)S(1)}, bf16[4096,896]{1,0:T(8,128)(2,1)}, u32[]{:S(2)}) copy-start(bf16[4096,896]{1,0:T(8,128)(2,1)} %dy_ref.1) | copy-start | bytes 22020100
  741.4 17.5 %copy-start = (bf16[2,2,2,2,2,304,896]{6,5,4,3,2,1,0:T(8,128)(2,1)S(1)}, bf16[2,2,2,2,2,304,896]{6,5,4,3,2,1,0:T(8,128)(2,1)}, u32[]{:S(2)}) copy-start(bf16[2,2,2,2,2,304,896]{6,5,4,3,2,1,0:T(8,128)(2,1)} %get-tuple-element.31) | copy-start | bytes 52297732
  758.9 8.8 %copy-start.6 = (f32[2,56,4864]{2,1,0:T(8,128)S(1)}, f32[2,56,4864]{2,1,0:T(8,128)}, u32[]{:S(2)}) copy-start(f32[2,56,4864]{2,1,0:T(8,128)} %get-tuple-element.52) | copy-start | bytes 6537220
  758.9 10.2 %copy-start.5 = (f32[2,304,896]{2,1,0:T(8,128)S(1)}, f32[2,304,896]{2,1,0:T(8,128)}, u32[]{:S(2)}) copy-start(f32[2,304,896]{2,1,0:T(8,128)} %get-tuple-element.53) | copy-start | bytes 6537220
  758.9 11.5 %copy-start.4 = (f32[2,56,4864]{2,1,0:T(8,128)S(1)}, f32[2,56,4864]{2,1,0:T(8,128)}, u32[]{:S(2)}) copy-start(f32[2,56,4864]{2,1,0:T(8,128)} %get-tuple-element.54) | copy-start | bytes 6537220
  758.9 12.9 %copy-start.3 = (f32[2,304,896]{2,1,0:T(8,128)S(1)}, f32[2,304,896]{2,1,0:T(8,128)}, u32[]{:S(2)}) copy-start(f32[2,304,896]{2,1,0:T(8,128)} %get-tuple-element.55) | copy-start | bytes 6537220
  767.7 5.4 copy-start.2
  767.7 6.7 copy-start.1

commit v4 on v3

--- a/solution.py
+++ b/solution.py
@@ -99,6 +99,10 @@
             return self.sums[held, 0] + self.landed[2][lax.rem(unit, SLOTS), 0]
 
 
+FLUSHES = TOKENS // BLOCK
+assert FLUSHES <= DRAIN + 1
+
+
 def within(unit, count):
     return jnp.logical_and(unit >= 0, unit < count)
 
@@ -126,16 +130,16 @@
     return pl.ds(pl.multiple_of(index * size, size), size)
 
 
-def grad_tile(z_ref, dy_ref, wd_ref, qbuf, extra):
+def grad_tile(z_ref, dy_ref, wd_ref, qbuf, size, extra):
     def block(index, carry):
-        rows = aligned(index, BLOCK)
+        rows = aligned(index, size)
         slope = gelu_parts(z_ref[rows, :])[1]
         grad = (dot_last(dy_ref[rows, :], wd_ref[...]) * slope).astype(BF16)
         qbuf[rows, :] = grad
         extra(rows, grad)
         return carry
 
-    lax.fori_loop(0, TOKENS // BLOCK, block, 0, unroll=TOKENS // BLOCK)
+    lax.fori_loop(0, TOKENS // size, block, 0, unroll=TOKENS // size)
 
 
 def store_tile(left, qbuf, gbuf, slot):
@@ -165,7 +169,7 @@
 
     @pl.when(step < STEPS)
     def _():
-        grad_tile(z_ref, dy_ref, wd_ref, qbuf, add_dx)
+        grad_tile(z_ref, dy_ref, wd_ref, qbuf, BLOCK // 2, add_dx)
         store_tile(left_ref, qbuf, up.gbuf, lax.rem(step, 2))
 
     def emit_up(unit, block):
@@ -187,24 +191,32 @@
         load(step).wait()
         down.copy(0, step).start()
 
-    @pl.when(step == STEPS - 1)
-    def _():
-        def flush(index, carry):
-            rows = aligned(index, BLOCK)
-            value = acc[rows, :]
-            stage_buf[...] = value.astype(BF16)
-            stage_t[...] = value.T.astype(BF16)
-            outs = [pltpu.make_async_copy(stage_buf, dx_ref.at[rows, :], out_sem.at[0]), pltpu.make_async_copy(stage_t, dxt_ref.at[:, rows], out_sem.at[1])]
-            for out in outs:
-                out.start()
-            for out in outs:
-                out.wait()
-            return carry
-
-        lax.fori_loop(0, TOKENS // BLOCK, flush, 0)
-
-
-def first_block_kernel(z_ref, dy_ref, wd_ref, dyt_ref, act_ref, x_ref, up_ref, down_ref, gd_ref, qbuf, left, stage_buf, *rest):
+    turn = step - (STEPS - 1)
+
+    def outs(index):
+        rows = aligned(index, BLOCK)
+        return [pltpu.make_async_copy(stage_buf, dx_ref.at[rows, :], out_sem.at[0]), pltpu.make_async_copy(stage_t, dxt_ref.at[:, rows], out_sem.at[1])]
+
+    @pl.when(jnp.logical_and(turn >= 1, turn < FLUSHES))
+    def _():
+        for copy in outs(turn - 1):
+            copy.wait()
+
+    @pl.when(within(turn, FLUSHES))
+    def _():
+        value = acc[aligned(turn, BLOCK), :]
+        stage_buf[...] = value.astype(BF16)
+        stage_t[...] = value.T.astype(BF16)
+        for copy in outs(turn):
+            copy.start()
+
+    @pl.when(turn == FLUSHES - 1)
+    def _():
+        for copy in outs(turn):
+            copy.wait()
+
+
+def first_block_kernel(z_ref, dy_ref, wd_ref, dyt_ref, act_ref, x_ref, up_ref, down_ref, gd_ref, qbuf, left, stage_buf, act_buf, act_sem, *rest):
     up = ReduceScatter(0, *rest[0:8])
     down = ReduceScatter(1, *rest[8:16])
     load_sem, out_sem = rest[16:18]
@@ -226,20 +238,34 @@
             return pltpu.make_async_copy(stage_buf.at[slot, :, pl.ds(0, SPLIT)], gd_ref.at[rows, pl.ds(0, SPLIT)], out_sem.at[slot])
         return pltpu.make_async_copy(stage_buf.at[slot, :, pl.ds(0, D - SPLIT)], gd_ref.at[rows, pl.ds(SPLIT, D - SPLIT)], out_sem.at[slot])
 
+    def fetch(index):
+        slot = lax.rem(index, ACT_SLOTS)
+        return pltpu.make_async_copy(act_ref.at[:, aligned(lax.rem(index, STEPS), TILE)], act_buf.at[slot], act_sem.at[slot])
+
     @pl.when(step == 0)
     def _():
+        for index in range(ACT_SLOTS):
+            fetch(index).start()
         greet_partners(up)
 
     @pl.when(step < TOKENS // TILE)
     def _():
         left[:, aligned(step, TILE)] = x_ref[...].T
+
+    @pl.when(step < 2 * STEPS)
+    def _():
+        fetch(step).wait()
 
     for split in (0, 1):
         @pl.when(within(step - split * STEPS, STEPS))
         def _():
             width = SPLIT if split == 0 else D - SPLIT
-            part = jnp.dot(dyt_ref[pl.ds(split * SPLIT, width), :], act_ref[...], preferred_element_type=F32)
+            part = jnp.dot(dyt_ref[pl.ds(split * SPLIT, width), :], act_buf[lax.rem(step, ACT_SLOTS)], preferred_element_type=F32)
             stage_buf[lax.rem(step, 2), :, pl.ds(0, width)] = part.T
+
+    @pl.when(step < 2 * STEPS - ACT_SLOTS)
+    def _():
+        fetch(step + ACT_SLOTS).start()
 
     for split in (0, 1):
         @pl.when(within(step - 1 - split * STEPS, STEPS))
@@ -255,7 +281,7 @@
 
     @pl.when(within(tile, STEPS))
     def _():
-        grad_tile(z_ref, dy_ref, wd_ref, qbuf, lambda rows, grad: None)
+        grad_tile(z_ref, dy_ref, wd_ref, qbuf, BLOCK, lambda rows, grad: None)
         store_tile(left, qbuf, up.gbuf, lax.rem(tile, 2))
 
     def emit_up(unit, block):
@@ -341,6 +367,7 @@
 DOWN_UNITS = 2 * D // LANES
 SPLIT = 512
 TICK_GAP = 4
+ACT_SLOTS = 3
 FIRST_TICK = STEPS + 3
 
 
@@ -354,12 +381,12 @@
             pl.BlockSpec((TOKENS, D), lambda s: (0, 0), pipeline_mode=WHOLE),
             pl.BlockSpec((None, TILE, D), lambda s: (0, jnp.clip(s - start, 0, last), 0)),
             pl.BlockSpec((D, TOKENS), lambda s: (0, 0), pipeline_mode=WHOLE),
-            pl.BlockSpec((TOKENS, TILE), lambda s: (0, lax.rem(jnp.minimum(s, start - 1), STEPS))),
+            ANY,
             pl.BlockSpec((TILE, D), lambda s: (jnp.minimum(s, TOKENS // TILE - 1), 0)),
         ],
         out_specs=[pl.BlockSpec((UP_ROWS, FF), lambda s: (0, 0)), pl.BlockSpec((DOWN_ROWS, D), lambda s: (0, 0)), ANY],
         out_shape=[jax.ShapeDtypeStruct((UP_ROWS, FF), F32), jax.ShapeDtypeStruct((DOWN_ROWS, D), F32), jax.ShapeDtypeStruct((FF, D), F32)],
-        scratch_shapes=[pltpu.VMEM((TOKENS, TILE), BF16), pltpu.VMEM((D, TOKENS), BF16), pltpu.VMEM((2, TILE, SPLIT), F32)] + ring_scratch(UP_ROWS, TILE) + ring_scratch(HALF_ROWS, LANES) + [pltpu.SemaphoreType.DMA((2, GROUP)), pltpu.SemaphoreType.DMA((2,))],
+        scratch_shapes=[pltpu.VMEM((TOKENS, TILE), BF16), pltpu.VMEM((D, TOKENS), BF16), pltpu.VMEM((2, TILE, SPLIT), F32), pltpu.VMEM((ACT_SLOTS, TOKENS, TILE), BF16), pltpu.SemaphoreType.DMA((ACT_SLOTS,))] + ring_scratch(UP_ROWS, TILE) + ring_scratch(HALF_ROWS, LANES) + [pltpu.SemaphoreType.DMA((2, GROUP)), pltpu.SemaphoreType.DMA((2,))],
         compiler_params=params(2),
         cost_estimate=pl.CostEstimate(flops=6 * TOKENS * D * FF, bytes_accessed=250 * 2**20, transcendentals=2 * TOKENS * FF),
     )(pre_act, grad, w_down, grad_t, act, act_in)

time: 785 us -> 771 us (0.982)
  Pallas kernels: 534 us -> 521 us
    pallas_call x1, Pallas kernels: 191 us -> 182 us  [second_block(): pl.pallas_call(second_block_kernel, grid=(STEPS + DRAIN,), in_specs=[pl.B...]
where the time goes in v4:
time: 771 us; the launch traced here: 763 us
  Pallas kernels  521 us (68%)
  matrix products  203 us (26%)
  local copies, waits for them, and re-layouts  35.6 us (5%)
    pallas_call x1, Pallas kernels, first_block(): pl.pallas_call(first_block_kernel, grid=(start + STEPS + DRAIN,), in_spec...  199 us
    pallas_call x1, Pallas kernels, second_block(): pl.pallas_call(second_block_kernel, grid=(STEPS + DRAIN,), in_specs=[pl.B...  182 us
    pallas_call x1, Pallas kernels, tail(): pl.pallas_call(tail_kernel, in_specs=[pl.BlockSpec(memory_space=pltpu.SME...  139 us
    dot_general x1, matrix products, device_step(): z_one = jnp.dot(act_in, w_up[0], preferred_element_type=F32)  59.3 us
    dot_general x1, matrix products, device_step(): z_three = jnp.dot(hidden, w_up[1], preferred_element_type=F32)  51 us
    dot_general x1, matrix products, device_step(): g_four = jnp.dot(act_three.T, grad_out, preferred_element_type=F32)  49.5 us
    dot_general x1, matrix products, device_step(): jnp.dot(act_one, w_down[0], preferred_element_type=F32).astype(BF16)  43.6 us
    unnamed x24, local copies, waits for them, and re-layouts  34.4 us

profile of v4, /device:TPU:0, one launch (start us, length us, event | category | flops | bytes accessed | tf_op | source)
XLA Modules:
  0.0 763.1 jit_solution(8687698789671391944)
XLA Ops:
  0.6 59.3 %multiply_convert_fusion.1 = (bf16[4096,4864]{1,0:T(8,128)(2,1)}, f32[4096,4864]{1,0:T(8,128)}) fusion(bf16[4096,896]{1,0:T(8,128)(2,1)} %x_ref.1, bf16[2,896,4864]{2,1,0:T(8,128)(2,1)} %wu_ref.1), kind=kOutput, calls=%fused_computation.1 | convolution fusion | flops 35801530368 | bytes 135593984 | tf_op jit(solution)/shard_map/dot_general | solution.py:562
  60.0 43.6 %fusion.10 = bf16[4096,896]{0,1:T(8,128)(2,1)} fusion(bf16[4096,4864]{1,0:T(8,128)(2,1)} %get-tuple-element.39.act_ref, bf16[2,4864,896]{2,1,0:T(8,128)(2,1)} %wd_ref.3), kind=kOutput, calls=%fused_computation.12 | convolution fusion | flops 35705585664 | bytes 55902208 | tf_op jit(solution)/shard_map/dot_general | solution.py:564
  103.5 0.0 copy-start.7
  103.5 51.0 %fusion.1.z_ref = f32[4096,4864]{1,0:T(8,128)} fusion(bf16[4096,896]{0,1:T(8,128)(2,1)} %fusion.10, bf16[2,896,4864]{2,1,0:T(8,128)(2,1)} %wu_ref.1), kind=kOutput, calls=%fused_computation.3 | convolution fusion | flops 35701915648 | bytes 95748096 | tf_op jit(solution)/shard_map/dot_general | solution.py:565
  154.5 0.0 copy-done.7
  154.5 49.5 %fusion = f32[4864,896]{1,0:T(8,128)} fusion(bf16[4096,896]{1,0:T(8,128)(2,1)S(1)} %copy-done.7, f32[4096,4864]{1,0:T(8,128)} %fusion.1.z_ref), kind=kOutput, calls=%fused_computation.2 | convolution fusion | flops 35801530368 | bytes 104464384 | tf_op jit(solution)/shard_map/dot_general | solution.py:567
  204.0 182.5 %shard_map.187 = (f32[56,4864]{1,0:T(8,128)}, f32[304,896]{1,0:T(8,128)}, bf16[4096,896]{1,0:T(8,128)(2,1)}, bf16[896,4096]{1,0:T(8,128)(2,1)}) custom-call(f32[4096,4864]{1,0:T(8,128)} %fusion.1.z_ref, bf16[4096,896]{1,0:T(8,128)(2,1)} %dy_ref.1, bf16[2,4864,896]{2,1,0:T(8,128)(2,1)} %wd_ref.3, bf16[896,4096]{1,0:T(8,128)(2,1)} %bitcast.36, ...), custom_call_target="tpu_custom_call" | custom-call | flops 107105746944 | bytes 157286400 | tf_op jit(solution)/shard_map/pallas_call | solution.py:346
  386.5 199.3 %shard_map.188 = (f32[56,4864]{1,0:T(8,128)}, f32[304,896]{1,0:T(8,128)}, f32[4864,896]{1,0:T(8,128)}) custom-call(f32[4096,4864]{1,0:T(8,128)} %get-tuple-element.40.z_ref, bf16[4096,896]{1,0:T(8,128)(2,1)} %get-tuple-element.24.dy_ref, bf16[2,4864,896]{2,1,0:T(8,128)(2,1)} %wd_ref.3, bf16[896,4096]{1,0:T(8,128)(2,1)} %get-tuple-element.25.dyt_ref, ...), custom_call_target="tpu_custom_call" | custom-call | flops 107105746944 | bytes 262144000 | tf_op jit(solution)/shard_map/pallas_call | solution.py:376
  587.1 0.6 pad_maximum_fusion.scalars
  587.7 139.3 %shard_map.189 = (bf16[2,2,2,2,2,56,4864]{6,5,4,3,2,1,0:T(8,128)(2,1)}, bf16[2,2,2,2,2,304,896]{6,5,4,3,2,1,0:T(8,128)(2,1)}, f32[2,56,4864]{2,1,0:T(8,128)}, f3...) custom-call(f32[2]{0:T(128)} %pad_maximum_fusion.scalars, ...), custom_call_target="tpu_custom_call" | custom-call | tf_op jit(solution)/shard_map/pallas_call | solution.py:535
  726.9 1.2 slice.15
  728.1 0.0 copy-start
  728.1 15.0 %copy.33 = bf16[2,896,4864]{2,1,0:T(8,128)(2,1)} copy(bf16[2,896,4864]{2,1,0:T(8,128)(2,1)} %bitcast.34) | data formatting | bytes 34865152
  743.1 2.5 copy-done
  745.6 0.0 copy-start.6
  745.6 0.0 copy-start.5
  745.6 0.0 copy-start.4
  745.6 0.0 copy-start.3
  745.6 8.8 %copy.34 = bf16[2,4864,896]{2,1,0:T(8,128)(2,1)} copy(bf16[2,4864,896]{2,1,0:T(8,128)(2,1)S(1)} %bitcast.33) | data formatting | bytes 34865152
  754.5 0.0 copy-done.6
  754.5 0.0 copy-start.2
  754.5 0.0 copy-start.1
  754.5 1.3 copy.35
  755.8 0.0 copy-done.5
  755.8 1.3 copy.36
  757.2 0.0 copy-done.4
  757.2 1.3 copy.37
  758.5 0.0 copy-done.3
  758.5 1.3 copy.38
  759.9 0.0 copy-done.2
  759.9 1.3 copy.39
  761.2 0.0 copy-done.1
  761.2 1.3 copy.40
Async XLA Ops:
  103.5 51.0 %copy-start.7 = (bf16[4096,896]{1,0:T(8,128)(2,1)S(1)}, bf16[4096,896]{1,0:T(8,128)(2,1)}, u32[]{:S(2)}) copy-start(bf16[4096,896]{1,0:T(8,128)(2,1)} %dy_ref.1) | copy-start | bytes 22020100
  728.1 17.5 %copy-start = (bf16[2,2,2,2,2,304,896]{6,5,4,3,2,1,0:T(8,128)(2,1)S(1)}, bf16[2,2,2,2,2,304,896]{6,5,4,3,2,1,0:T(8,128)(2,1)}, u32[]{:S(2)}) copy-start(bf16[2,2,2,2,2,304,896]{6,5,4,3,2,1,0:T(8,128)(2,1)} %get-tuple-element.31) | copy-start | bytes 52297732
  745.6 8.8 %copy-start.6 = (f32[2,56,4864]{2,1,0:T(8,128)S(1)}, f32[2,56,4864]{2,1,0:T(8,128)}, u32[]{:S(2)}) copy-start(f32[2,56,4864]{2,1,0:T(8,128)} %get-tuple-element.52) | copy-start | bytes 6537220
  745.6 10.2 %copy-start.5 = (f32[2,304,896]{2,1,0:T(8,128)S(1)}, f32[2,304,896]{2,1,0:T(8,128)}, u32[]{:S(2)}) copy-start(f32[2,304,896]{2,1,0:T(8,128)} %get-tuple-element.53) | copy-start | bytes 6537220
  745.6 11.5 %copy-start.4 = (f32[2,56,4864]{2,1,0:T(8,128)S(1)}, f32[2,56,4864]{2,1,0:T(8,128)}, u32[]{:S(2)}) copy-start(f32[2,56,4864]{2,1,0:T(8,128)} %get-tuple-element.54) | copy-start | bytes 6537220
  745.6 12.9 %copy-start.3 = (f32[2,304,896]{2,1,0:T(8,128)S(1)}, f32[2,304,896]{2,1,0:T(8,128)}, u32[]{:S(2)}) copy-start(f32[2,304,896]{2,1,0:T(8,128)} %get-tuple-element.55) | copy-start | bytes 6537220
  754.5 5.4 copy-start.2
  754.5 6.7 copy-start.1

commit v5 on v4

--- a/solution.py
+++ b/solution.py
@@ -231,16 +231,13 @@
             copies.append(pltpu.make_async_copy(gd_ref.at[rows, columns], down.gbuf.at[slot, i // 2, i % 2], load_sem.at[slot, i]))
         return copies
 
-    def write(index, split):
+    def write(index):
         slot = lax.rem(index, 2)
-        rows = aligned(lax.rem(index, STEPS), TILE)
-        if split == 0:
-            return pltpu.make_async_copy(stage_buf.at[slot, :, pl.ds(0, SPLIT)], gd_ref.at[rows, pl.ds(0, SPLIT)], out_sem.at[slot])
-        return pltpu.make_async_copy(stage_buf.at[slot, :, pl.ds(0, D - SPLIT)], gd_ref.at[rows, pl.ds(SPLIT, D - SPLIT)], out_sem.at[slot])
+        return pltpu.make_async_copy(stage_buf.at[slot], gd_ref.at[aligned(index, TILE), :], out_sem.at[slot])
 
     def fetch(index):
         slot = lax.rem(index, ACT_SLOTS)
-        return pltpu.make_async_copy(act_ref.at[:, aligned(lax.rem(index, STEPS), TILE)], act_buf.at[slot], act_sem.at[slot])
+        return pltpu.make_async_copy(act_ref.at[:, aligned(index, TILE)], act_buf.at[slot], act_sem.at[slot])
 
     @pl.when(step == 0)
     def _():
@@ -252,32 +249,25 @@
     def _():
         left[:, aligned(step, TILE)] = x_ref[...].T
 
-    @pl.when(step < 2 * STEPS)
+    @pl.when(step < STEPS)
     def _():
         fetch(step).wait()
-
-    for split in (0, 1):
-        @pl.when(within(step - split * STEPS, STEPS))
-        def _():
-            width = SPLIT if split == 0 else D - SPLIT
-            part = jnp.dot(dyt_ref[pl.ds(split * SPLIT, width), :], act_buf[lax.rem(step, ACT_SLOTS)], preferred_element_type=F32)
-            stage_buf[lax.rem(step, 2), :, pl.ds(0, width)] = part.T
-
-    @pl.when(step < 2 * STEPS - ACT_SLOTS)
+        part = jnp.dot(dyt_ref[...], act_buf[lax.rem(step, ACT_SLOTS)], preferred_element_type=F32)
+        stage_buf[lax.rem(step, 2)] = part.T
+
+    @pl.when(step < STEPS - ACT_SLOTS)
     def _():
         fetch(step + ACT_SLOTS).start()
 
-    for split in (0, 1):
-        @pl.when(within(step - 1 - split * STEPS, STEPS))
-        def _():
-            write(step - 1, split).wait()
-
-    for split in (0, 1):
-        @pl.when(within(step - split * STEPS, STEPS))
-        def _():
-            write(step, split).start()
-
-    tile = step - 2 * STEPS
+    @pl.when(within(step - 1, STEPS))
+    def _():
+        write(step - 1).wait()
+
+    @pl.when(step < STEPS)
+    def _():
+        write(step).start()
+
+    tile = step - STEPS
 
     @pl.when(within(tile, STEPS))
     def _():
@@ -290,15 +280,12 @@
     def emit_down(unit, block):
         down_ref[pl.ds(pl.multiple_of(lax.rem(unit, 2) * HALF_ROWS, 8), HALF_ROWS), aligned(unit // 2, LANES)] = block
 
-    early = step - FIRST_TICK
-    ticking = jnp.logical_or(jnp.logical_and(early >= 0, lax.rem(early, TICK_GAP) == 0), tile >= 0)
-    tick = jnp.where(tile >= 0, tile + (2 * STEPS - FIRST_TICK) // TICK_GAP, early // TICK_GAP)
-    tick = jnp.where(ticking, tick, -1)
+    tick = tile - 1
 
     advance(up, tile, STEPS, emit_up)
     advance(down, tick, DOWN_UNITS, emit_down)
 
-    @pl.when(step == FIRST_TICK - 1)
+    @pl.when(tile == 0)
     def _():
         for copy in loads(0):
             copy.start()
@@ -365,14 +352,11 @@
 LANES = 128
 HALF_ROWS = DOWN_ROWS // 2
 DOWN_UNITS = 2 * D // LANES
-SPLIT = 512
-TICK_GAP = 4
-ACT_SLOTS = 3
-FIRST_TICK = STEPS + 3
+ACT_SLOTS = 2
 
 
 def first_block(pre_act, grad, w_down, grad_t, act, act_in):
-    start, last = 2 * STEPS, STEPS - 1
+    start, last = STEPS, STEPS - 1
     return pl.pallas_call(
         first_block_kernel,
         grid=(start + STEPS + DRAIN,),
@@ -386,7 +370,7 @@
         ],
         out_specs=[pl.BlockSpec((UP_ROWS, FF), lambda s: (0, 0)), pl.BlockSpec((DOWN_ROWS, D), lambda s: (0, 0)), ANY],
         out_shape=[jax.ShapeDtypeStruct((UP_ROWS, FF), F32), jax.ShapeDtypeStruct((DOWN_ROWS, D), F32), jax.ShapeDtypeStruct((FF, D), F32)],
-        scratch_shapes=[pltpu.VMEM((TOKENS, TILE), BF16), pltpu.VMEM((D, TOKENS), BF16), pltpu.VMEM((2, TILE, SPLIT), F32), pltpu.VMEM((ACT_SLOTS, TOKENS, TILE), BF16), pltpu.SemaphoreType.DMA((ACT_SLOTS,))] + ring_scratch(UP_ROWS, TILE) + ring_scratch(HALF_ROWS, LANES) + [pltpu.SemaphoreType.DMA((2, GROUP)), pltpu.SemaphoreType.DMA((2,))],
+        scratch_shapes=[pltpu.VMEM((TOKENS, TILE), BF16), pltpu.VMEM((D, TOKENS), BF16), pltpu.VMEM((2, TILE, D), F32), pltpu.VMEM((ACT_SLOTS, TOKENS, TILE), BF16), pltpu.SemaphoreType.DMA((ACT_SLOTS,))] + ring_scratch(UP_ROWS, TILE) + ring_scratch(HALF_ROWS, LANES) + [pltpu.SemaphoreType.DMA((2, GROUP)), pltpu.SemaphoreType.DMA((2,))],
         compiler_params=params(2),
         cost_estimate=pl.CostEstimate(flops=6 * TOKENS * D * FF, bytes_accessed=250 * 2**20, transcendentals=2 * TOKENS * FF),
     )(pre_act, grad, w_down, grad_t, act, act_in)

time: 771 us -> 785 us (1.018)
  Pallas kernels: 521 us -> 535 us
    pallas_call x1, Pallas kernels: 199 us -> 214 us  [first_block(): pl.pallas_call(first_block_kernel, grid=(start + STEPS + DRAIN,), in_spec...]
where the time goes in v5:
time: 785 us; the launch traced here: 777 us
  Pallas kernels  535 us (68%)
  matrix products  203 us (26%)
  local copies, waits for them, and re-layouts  35.6 us (5%)
    pallas_call x1, Pallas kernels, first_block(): pl.pallas_call(first_block_kernel, grid=(start + STEPS + DRAIN,), in_spec...  214 us
    pallas_call x1, Pallas kernels, second_block(): pl.pallas_call(second_block_kernel, grid=(STEPS + DRAIN,), in_specs=[pl.B...  182 us
    pallas_call x1, Pallas kernels, tail(): pl.pallas_call(tail_kernel, in_specs=[pl.BlockSpec(memory_space=pltpu.SME...  139 us
    dot_general x1, matrix products, device_step(): z_one = jnp.dot(act_in, w_up[0], preferred_element_type=F32)  59.3 us
    dot_general x1, matrix products, device_step(): z_three = jnp.dot(hidden, w_up[1], preferred_element_type=F32)  51 us
    dot_general x1, matrix products, device_step(): g_four = jnp.dot(act_three.T, grad_out, preferred_element_type=F32)  49.5 us
    dot_general x1, matrix products, device_step(): jnp.dot(act_one, w_down[0], preferred_element_type=F32).astype(BF16)  43.6 us
    unnamed x24, local copies, waits for them, and re-layouts  34.4 us

profile of v5, /device:TPU:0, one launch (start us, length us, event | category | flops | bytes accessed | tf_op | source)
XLA Modules:
  0.0 777.1 jit_solution(13886914616406016361)
XLA Ops:
  0.6 59.3 %multiply_convert_fusion.1 = (bf16[4096,4864]{1,0:T(8,128)(2,1)}, f32[4096,4864]{1,0:T(8,128)}) fusion(bf16[4096,896]{1,0:T(8,128)(2,1)} %x_ref.1, bf16[2,896,4864]{2,1,0:T(8,128)(2,1)} %wu_ref.1), kind=kOutput, calls=%fused_computation.1 | convolution fusion | flops 35801530368 | bytes 135593984 | tf_op jit(solution)/shard_map/dot_general | solution.py:546
  60.0 43.6 %fusion.10 = bf16[4096,896]{0,1:T(8,128)(2,1)} fusion(bf16[4096,4864]{1,0:T(8,128)(2,1)} %get-tuple-element.39.act_ref, bf16[2,4864,896]{2,1,0:T(8,128)(2,1)} %wd_ref.3), kind=kOutput, calls=%fused_computation.12 | convolution fusion | flops 35705585664 | bytes 55902208 | tf_op jit(solution)/shard_map/dot_general | solution.py:548
  103.5 0.0 copy-start.7
  103.5 51.0 %fusion.1.z_ref = f32[4096,4864]{1,0:T(8,128)} fusion(bf16[4096,896]{0,1:T(8,128)(2,1)} %fusion.10, bf16[2,896,4864]{2,1,0:T(8,128)(2,1)} %wu_ref.1), kind=kOutput, calls=%fused_computation.3 | convolution fusion | flops 35701915648 | bytes 95748096 | tf_op jit(solution)/shard_map/dot_general | solution.py:549
  154.5 0.0 copy-done.7
  154.5 49.5 %fusion = f32[4864,896]{1,0:T(8,128)} fusion(bf16[4096,896]{1,0:T(8,128)(2,1)S(1)} %copy-done.7, f32[4096,4864]{1,0:T(8,128)} %fusion.1.z_ref), kind=kOutput, calls=%fused_computation.2 | convolution fusion | flops 35801530368 | bytes 104464384 | tf_op jit(solution)/shard_map/dot_general | solution.py:551
  204.0 182.5 %shard_map.187 = (f32[56,4864]{1,0:T(8,128)}, f32[304,896]{1,0:T(8,128)}, bf16[4096,896]{1,0:T(8,128)(2,1)}, bf16[896,4096]{1,0:T(8,128)(2,1)}) custom-call(f32[4096,4864]{1,0:T(8,128)} %fusion.1.z_ref, bf16[4096,896]{1,0:T(8,128)(2,1)} %dy_ref.1, bf16[2,4864,896]{2,1,0:T(8,128)(2,1)} %wd_ref.3, bf16[896,4096]{1,0:T(8,128)(2,1)} %bitcast.36, ...), custom_call_target="tpu_custom_call" | custom-call | flops 107105746944 | bytes 157286400 | tf_op jit(solution)/shard_map/pallas_call | solution.py:333
  386.5 213.6 %shard_map.188 = (f32[56,4864]{1,0:T(8,128)}, f32[304,896]{1,0:T(8,128)}, f32[4864,896]{1,0:T(8,128)}) custom-call(f32[4096,4864]{1,0:T(8,128)} %get-tuple-element.40.z_ref, bf16[4096,896]{1,0:T(8,128)(2,1)} %get-tuple-element.24.dy_ref, bf16[2,4864,896]{2,1,0:T(8,128)(2,1)} %wd_ref.3, bf16[896,4096]{1,0:T(8,128)(2,1)} %get-tuple-element.25.dyt_ref, ...), custom_call_target="tpu_custom_call" | custom-call | flops 107105746944 | bytes 262144000 | tf_op jit(solution)/shard_map/pallas_call | solution.py:360
  601.4 0.6 pad_maximum_fusion.scalars
  602.0 139.0 %shard_map.189 = (bf16[2,2,2,2,2,56,4864]{6,5,4,3,2,1,0:T(8,128)(2,1)}, bf16[2,2,2,2,2,304,896]{6,5,4,3,2,1,0:T(8,128)(2,1)}, f32[2,56,4864]{2,1,0:T(8,128)}, f3...) custom-call(f32[2]{0:T(128)} %pad_maximum_fusion.scalars, ...), custom_call_target="tpu_custom_call" | custom-call | tf_op jit(solution)/shard_map/pallas_call | solution.py:519
  741.0 1.2 slice.15
  742.2 0.0 copy-start
  742.2 15.0 %copy.33 = bf16[2,896,4864]{2,1,0:T(8,128)(2,1)} copy(bf16[2,896,4864]{2,1,0:T(8,128)(2,1)} %bitcast.34) | data formatting | bytes 34865152
  757.1 2.5 copy-done
  759.7 0.0 copy-start.6
  759.7 0.0 copy-start.5
  759.7 0.0 copy-start.4
  759.7 0.0 copy-start.3
  759.7 8.8 %copy.34 = bf16[2,4864,896]{2,1,0:T(8,128)(2,1)} copy(bf16[2,4864,896]{2,1,0:T(8,128)(2,1)S(1)} %bitcast.33) | data formatting | bytes 34865152
  768.5 0.0 copy-done.6
  768.5 0.0 copy-start.2
  768.5 0.0 copy-start.1
  768.5 1.3 copy.35
  769.9 0.0 copy-done.5
  769.9 1.3 copy.36
  771.2 0.0 copy-done.4
  771.2 1.3 copy.37
  772.6 0.0 copy-done.3
  772.6 1.3 copy.38
  773.9 0.0 copy-done.2
  773.9 1.3 copy.39
  775.3 0.0 copy-done.1
  775.3 1.3 copy.40
Async XLA Ops:
  103.5 51.0 %copy-start.7 = (bf16[4096,896]{1,0:T(8,128)(2,1)S(1)}, bf16[4096,896]{1,0:T(8,128)(2,1)}, u32[]{:S(2)}) copy-start(bf16[4096,896]{1,0:T(8,128)(2,1)} %dy_ref.1) | copy-start | bytes 22020100
  742.2 17.5 %copy-start = (bf16[2,2,2,2,2,304,896]{6,5,4,3,2,1,0:T(8,128)(2,1)S(1)}, bf16[2,2,2,2,2,304,896]{6,5,4,3,2,1,0:T(8,128)(2,1)}, u32[]{:S(2)}) copy-start(bf16[2,2,2,2,2,304,896]{6,5,4,3,2,1,0:T(8,128)(2,1)} %get-tuple-element.31) | copy-start | bytes 52297732
  759.7 8.8 %copy-start.6 = (f32[2,56,4864]{2,1,0:T(8,128)S(1)}, f32[2,56,4864]{2,1,0:T(8,128)}, u32[]{:S(2)}) copy-start(f32[2,56,4864]{2,1,0:T(8,128)} %get-tuple-element.52) | copy-start | bytes 6537220
  759.7 10.2 %copy-start.5 = (f32[2,304,896]{2,1,0:T(8,128)S(1)}, f32[2,304,896]{2,1,0:T(8,128)}, u32[]{:S(2)}) copy-start(f32[2,304,896]{2,1,0:T(8,128)} %get-tuple-element.53) | copy-start | bytes 6537220
  759.7 11.5 %copy-start.4 = (f32[2,56,4864]{2,1,0:T(8,128)S(1)}, f32[2,56,4864]{2,1,0:T(8,128)}, u32[]{:S(2)}) copy-start(f32[2,56,4864]{2,1,0:T(8,128)} %get-tuple-element.54) | copy-start | bytes 6537220
  759.7 12.9 %copy-start.3 = (f32[2,304,896]{2,1,0:T(8,128)S(1)}, f32[2,304,896]{2,1,0:T(8,128)}, u32[]{:S(2)}) copy-start(f32[2,304,896]{2,1,0:T(8,128)} %get-tuple-element.55) | copy-start | bytes 6537220
  768.5 5.4 copy-start.2
  768.5 6.7 copy-start.1
